TPU v7x, 256 devices: a whole 4x4x8 slice. The times are simulated.
256 devices in a mesh: outer: 16 (over x_lo, y, core), inner: 16 (over z, x_hi).
Axes of the slice: x: 4 (x_hi: 2, x_lo: 2; x = x_hi * 2 + x_lo), y: 4, z: 8, core: 2. Of those that a mesh axis runs over, the one named last changes fastest.
Arguments:
- query_image: bfloat16 [8192, 2048], P(('outer', 'inner')), may hold values from -6 to 6
- key_image: bfloat16 [8192, 2048], P(('outer', 'inner')), may hold values from -6 to 6
- value_image: bfloat16 [8192, 2048], P(('outer', 'inner')), may hold values from -6 to 6
- attended_image: bfloat16 [8192, 2048], P(('outer', 'inner')), may hold values from -6 to 6
- upstream_image: bfloat16 [8192, 2048], P(('outer', 'inner')), may hold values from -128 to 128
- logsum_image: float32 [8192, 16], P(('outer', 'inner')), may hold values from 8.6 to 9.4
- query_text: bfloat16 [512, 2048], P(None, 'outer'), may hold values from -6 to 6
- key_text: bfloat16 [512, 2048], P(None, 'outer'), may hold values from -6 to 6
- value_text: bfloat16 [512, 2048], P(None, 'outer'), may hold values from -6 to 6
- attended_text: bfloat16 [512, 2048], P(None, 'outer'), may hold values from -6 to 6
- upstream_text: bfloat16 [512, 2048], P(None, 'outer'), may hold values from -128 to 128
- logsum_text: float32 [512, 16], P(None, 'outer'), may hold values from 8.6 to 9.4
Outputs:
- grad_query_image: bfloat16 [8192, 2048], P(('outer', 'inner'))
- grad_key_image: bfloat16 [8192, 2048], P(('outer', 'inner'))
- grad_value_image: bfloat16 [8192, 2048], P(('outer', 'inner'))
- grad_query_text: bfloat16 [512, 2048], P('inner', 'outer')
- grad_key_text: bfloat16 [512, 2048], P('inner', 'outer')
- grad_value_text: bfloat16 [512, 2048], P('inner', 'outer')
All inputs are finite; a program needn't handle non-finite values.
Results may differ from a plain program's by a relative error of at most 0.0055.
Values may be sent and summed in bfloat16 or wider, within the bound.
No kernel may reach another device: no remote copies, remote signals or barrier semaphores. Data moves between devices by JAX's collectives and lax.ppermute only.
A program may use at most 64 MiB of HBM per device.

v0:
```python
import functools

import jax
import jax.numpy as jnp
from jax import lax
from jax.experimental import pallas as pl
from jax.experimental.pallas import tpu as pltpu
from jax.sharding import PartitionSpec as P


HEAD_DIM = 128
HEADS = 16
RING = 8
TOK = 32
NEAR = 512
OWN = NEAR + TOK
CHUNK = 136
SCALE = HEAD_DIM**-0.5
LOG2E = 1.4426950408889634
F32 = jnp.float32
BF16 = jnp.bfloat16
VMEM_LIMIT = 24 << 20
WHOLE_VMEM = 62 << 20
VM = pl.BlockSpec(memory_space=pltpu.VMEM)
HB = pl.BlockSpec(memory_space=pltpu.HBM)


def nt(a, b):
    return lax.dot_general(a, b, (((1,), (1,)), ((), ())), preferred_element_type=F32)


def nn(a, b):
    return lax.dot_general(a, b, (((1,), (0,)), ((), ())), preferred_element_type=F32)


def tn(a, b):
    return lax.dot_general(a, b, (((0,), (0,)), ((), ())), preferred_element_type=F32)


def three_pieces(x):
    first = x.astype(BF16)
    rest = x - first.astype(F32)
    second = rest.astype(BF16)
    third = (rest - second.astype(F32)).astype(BF16)
    return first.astype(F32), second.astype(F32), third.astype(F32)


def place():
    inner = lax.axis_index("inner")
    return inner // 2, lax.rem(inner, 2)


def pack_body(q_in, k_in, v_in, o_in, g_in, logs, out, rows, q, k, v, o, g, sems):
    copies = [
        pltpu.make_async_copy(source, target, sems.at[n])
        for n, (source, target) in enumerate(((g_in, g), (o_in, o), (q_in, q), (k_in, k), (v_in, v)))
    ]
    for copy in copies:
        copy.start()
    for copy in copies:
        copy.wait()
    slot = lax.rem(lax.axis_index("outer"), 4)
    lane_head = lax.broadcasted_iota(jnp.int32, (TOK, 128), 1)
    sums = jnp.zeros((TOK, 128), F32)
    for h in range(HEADS):
        cols = slice(h * 128, (h + 1) * 128)
        out[h, 0:32, :] = q[:, cols]
        out[h, 32:64, :] = g[:, cols]
        out[h, 64:96, :] = k[:, cols]
        out[h, 96:128, :] = v[:, cols]
        product = g[:, cols].astype(F32) * o[:, cols].astype(F32)
        sums = jnp.where(lane_head == h, jnp.sum(product, axis=1, keepdims=True), sums)
    deltas = jnp.transpose(jnp.concatenate([sums] * 4, axis=0))[0:HEADS]
    logs4 = jnp.concatenate([logs[...] * LOG2E] * 4, axis=1)
    mine = lax.broadcasted_iota(jnp.int32, (HEADS, 128), 1) // TOK == slot
    pieces = three_pieces(jnp.where(mine, logs4, 0.0)) + three_pieces(jnp.where(mine, deltas, 0.0))
    rows[...] = jnp.zeros_like(rows)
    for h in range(HEADS):
        for n, piece in enumerate(pieces):
            rows[h, n : n + 1, :] = piece[h : h + 1, :]
    for h in range(HEADS):
        out[h, 128:136, :] = rows[h].astype(BF16)


def unpack_body(got, qg, kv):
    for o in range(HEADS):
        qg[o * TOK : (o + 1) * TOK, :] = got[o, 0:32, :]
        qg[NEAR + o * TOK : NEAR + (o + 1) * TOK, :] = got[o, 32:64, :]
        kv[o * TOK : (o + 1) * TOK, :] = got[o, 64:96, :]
        kv[NEAR + o * TOK : NEAR + (o + 1) * TOK, :] = got[o, 96:128, :]
    for a in range(4):
        total = got[4 * a, 128:136, :].astype(F32)
        for j in range(1, 4):
            total = total + got[4 * a + j, 128:136, :].astype(F32)
        qg[2 * NEAR + 8 * a : 2 * NEAR + 8 * a + 8, :] = total.astype(BF16)


def one_block(q, g, logs, deltas, keys, values, dk, dv):
    total = None
    for base, size in ((0, NEAR), (NEAR, 2 * OWN - NEAR)):
        k, v = keys[base : base + size, :], values[base : base + size, :]
        weights = jnp.exp2(nt(k, q) * (SCALE * LOG2E) - logs)
        mixed = (weights * (nt(v, g) - deltas)).astype(BF16)
        dv[base : base + size, :] += nn(weights.astype(BF16), g)
        dk[base : base + size, :] += nn(mixed, q)
        part = tn(mixed, k)
        total = part if total is None else total + part
    return total * SCALE


def block_operands(qg):
    ld = qg[2 * NEAR : 2 * NEAR + 32, :].astype(F32)
    logs = jnp.concatenate(
        [ld[8 * a : 8 * a + 1] + ld[8 * a + 1 : 8 * a + 2] + ld[8 * a + 2 : 8 * a + 3] for a in range(4)],
        axis=1,
    )
    deltas = jnp.concatenate(
        [ld[8 * a + 3 : 8 * a + 4] + ld[8 * a + 4 : 8 * a + 5] + ld[8 * a + 5 : 8 * a + 6] for a in range(4)],
        axis=1,
    )
    return qg[0:NEAR, :], qg[NEAR : 2 * NEAR, :], logs, deltas


def text_body(kv_own, kv_other, text_k, text_v, text_q, text_g, text_ld, dq_text, dk, dv, keys, values, tq, tg):
    z, side = place()
    for target, start, text in ((keys, 0, text_k), (values, NEAR, text_v)):
        target[0:NEAR, :] = kv_own[start : start + NEAR, :]
        target[NEAR : 2 * NEAR, :] = kv_other[start : start + NEAR, :]
        target[2 * NEAR : 2 * OWN, :] = text[pl.ds(pl.multiple_of(z * 64, 64), 2 * TOK), :]
    dk[...] = jnp.zeros_like(dk)
    dv[...] = jnp.zeros_like(dv)
    for n in range(RING):
        rows = pl.ds(pl.multiple_of(n * 64 + side * TOK, TOK), TOK)
        tq[n * TOK : (n + 1) * TOK, :] = text_q[rows, :]
        tg[n * TOK : (n + 1) * TOK, :] = text_g[rows, :]
    logs, deltas = text_ld[pl.ds(side, 1), :], text_ld[pl.ds(2 + side, 1), :]
    dq_text[...] = one_block(tq[...], tg[...], logs, deltas, keys, values, dk, dv).astype(BF16)


def own_body(keys, values, qg, dk_in, dv_in, dq, dk, dv):
    dk[...] = dk_in[...]
    dv[...] = dv_in[...]
    q, g, logs, deltas = block_operands(qg)
    dq[...] = one_block(q, g, logs, deltas, keys, values, dk, dv)


def far_body(step, *refs):
    keys, values, dq_text = refs[:3]
    z, side = place()
    count = 2 if step < 4 else 1
    blocks, refs = refs[3 : 3 + count], refs[3 + count :]
    (dk_in, dv_in), refs = refs[:2], refs[2:]
    if step == 3:
        firsts, refs = refs[:2], refs[2:]
    dqs, refs = refs[:count], refs[count:]
    (dk, dv), refs = refs[:2], refs[2:]
    dk[...] = dk_in[...]
    dv[...] = dv_in[...]
    for n, (qg, dq) in enumerate(zip(blocks, dqs)):
        q, g, logs, deltas = block_operands(qg)
        dq[0:NEAR, :] = one_block(q, g, logs, deltas, keys, values, dk, dv).astype(dq.dtype)
        owner = lax.rem(z + (step if n == 1 else RING - step), RING)
        text = dq_text[pl.ds(pl.multiple_of(owner * TOK, TOK), TOK), :]
        dq[NEAR:OWN, :] = text.astype(dq.dtype)
        if step == 3:
            dq[OWN : 2 * OWN, :] = firsts[n][...]
    if step == 4:
        (send,) = refs
        text = pl.ds(pl.multiple_of(2 * NEAR + (1 - side) * TOK, TOK), TOK)
        for source, lanes, factor in ((dk, slice(0, 128), SCALE), (dv, slice(128, 256), 1.0)):
            send[0:NEAR, lanes] = (source[NEAR : 2 * NEAR, :] * factor).astype(BF16)
            send[NEAR:OWN, lanes] = (source[text, :] * factor).astype(BF16)


def mid_body(mine, *refs):
    total = mine[...]
    for got in refs[:-1]:
        total = total + got[0:OWN, :].astype(F32)
    refs[-1][...] = total.astype(BF16)


def join_body(dq, dq_text, dk, dv, kv_got, from_low, from_high, *refs):
    gots = refs[:2]
    out, out_q, out_k, out_v = refs[2:]
    z, side = place()

    def arrived(total, start, size):
        for got, base in ((from_low, OWN), (from_high, OWN), *((got, 0) for got in gots)):
            total = total + got[base + start : base + start + size, :].astype(F32)
        return total.astype(BF16)

    for o in range(HEADS):
        at = slice(o * TOK, (o + 1) * TOK)
        out[o, 0:32, :] = arrived(dq[at, :], o * TOK, TOK)
        out[o, 32:64, :] = (dk[at, :] * SCALE + kv_got[at, 0:128].astype(F32)).astype(BF16)
        out[o, 64:96, :] = (dv[at, :] + kv_got[at, 128:256].astype(F32)).astype(BF16)
    own_text = dq_text[pl.ds(pl.multiple_of(z * TOK, TOK), TOK), :].astype(F32)
    out_q[...] = arrived(own_text, NEAR, TOK)
    text = pl.ds(pl.multiple_of(2 * NEAR + side * TOK, TOK), TOK)
    out_k[...] = (dk[text, :] * SCALE + kv_got[NEAR:OWN, 0:128].astype(F32)).astype(BF16)
    out_v[...] = (dv[text, :] + kv_got[NEAR:OWN, 128:256].astype(F32)).astype(BF16)


def spread_body(got, dq, dk, dv):
    for h in range(HEADS):
        cols = slice(h * 128, (h + 1) * 128)
        dq[:, cols] = got[h, 0:32, :]
        dk[:, cols] = got[h, 32:64, :]
        dv[:, cols] = got[h, 64:96, :]


def kernel(body, outs, count, flops=0, scratch=(), aliases=None, limit=VMEM_LIMIT):
    return pl.pallas_call(
        body,
        out_shape=outs,
        in_specs=count if isinstance(count, list) else [VM] * count,
        out_specs=jax.tree.map(lambda _: VM, outs),
        scratch_shapes=scratch,
        input_output_aliases=aliases or {},
        cost_estimate=pl.CostEstimate(flops=flops, bytes_accessed=1 << 20, transcendentals=0),
        compiler_params=pltpu.CompilerParams(vmem_limit_bytes=limit),
    )


def sds(shape, dtype=BF16):
    return jax.ShapeDtypeStruct(shape, dtype)


def block_flops(queries):
    return 10 * queries * 2 * OWN * HEAD_DIM


def shards(
    query_image,
    key_image,
    value_image,
    attended_image,
    upstream_image,
    logsum_image,
    query_text,
    key_text,
    value_text,
    attended_text,
    upstream_text,
    logsum_text,
):
    def along_ring(x, step):
        pairs = [(2 * z + side, 2 * ((z + step) % RING) + side) for z in range(RING) for side in range(2)]
        return lax.ppermute(x, "inner", pairs)

    def exchanged(x):
        return lax.all_to_all(x, "outer", split_axis=0, concat_axis=0, tiled=True)

    def across(x):
        return lax.ppermute(x, "inner", [(n, n ^ 1) for n in range(2 * RING)])

    packed = kernel(
        pack_body,
        sds((HEADS, CHUNK, 128)),
        [HB] * 5 + [VM],
        scratch=[pltpu.VMEM((HEADS, 8, 128), F32)]
        + [pltpu.VMEM((TOK, HEADS * 128), BF16)] * 5
        + [pltpu.SemaphoreType.DMA((5,))],
        limit=WHOLE_VMEM,
    )(query_image, key_image, value_image, attended_image, upstream_image, logsum_image.T)
    got = exchanged(packed)
    qg, kv = kernel(unpack_body, [sds((2 * NEAR + 32, 128)), sds((2 * NEAR, 128))], 1)(got)

    text_delta = jnp.sum(upstream_text.astype(F32) * attended_text.astype(F32), axis=1)
    text_ld = jnp.stack([logsum_text[:, 0] * LOG2E, text_delta]).reshape(2, RING, 2, TOK)
    text_ld = text_ld.transpose(0, 2, 1, 3).reshape(4, RING * TOK)

    kv_other = across(kv)
    acc = sds((2 * OWN, 128), F32)
    dq_text, dk, dv, keys, values = kernel(
        text_body,
        [sds((RING * TOK, 128)), acc, acc, sds((2 * OWN, 128)), sds((2 * OWN, 128))],
        7,
        flops=block_flops(RING * TOK),
        scratch=[pltpu.VMEM((RING * TOK, 128), BF16)] * 2,
    )(kv, kv_other, key_text, value_text, query_text, upstream_text, text_ld)

    up = down = qg
    parts = {}
    for step in range(1, 5):
        up = along_ring(up, 1)
        blocks = [up]
        if step < 4:
            down = along_ring(down, -1)
            blocks.append(down)
        count = len(blocks)
        part = {1: sds((OWN, 128)), 2: sds((OWN, 128), F32), 3: sds((2 * OWN, 128)), 4: sds((OWN, 128))}[step]
        result = kernel(
            functools.partial(far_body, step),
            [part] * count + [acc, acc] + ([sds((OWN, 256))] if step == 4 else []),
            5 + count + (2 if step == 3 else 0),
            flops=block_flops(NEAR * count),
            aliases={3 + count: count, 4 + count: count + 1},
        )(keys, values, dq_text, *blocks, dk, dv, *(parts[1] if step == 3 else ()))
        parts[step] = result[:count]
        dk, dv = result[count : count + 2]
        if step == 2:
            dq, dk, dv = kernel(
                own_body, [sds((NEAR, 128), F32), acc, acc], 5, flops=block_flops(NEAR), aliases={3: 1, 4: 2}
            )(keys, values, qg, dk, dv)
    kv_got = across(result[-1])
    from_high = along_ring(parts[3][0], -1)
    from_low = along_ring(parts[3][1], 1)
    from_far = along_ring(parts[4][0], -2)
    low, high = parts[2]
    high = kernel(mid_body, sds((OWN, 128)), 2)(high, from_low)
    back2 = along_ring(high, 2)
    low = kernel(mid_body, sds((OWN, 128)), 3)(low, from_high, from_far)
    back6 = along_ring(low, -2)

    joined, text_dq, text_dk, text_dv = kernel(
        join_body, [sds((HEADS, 96, 128)), sds((TOK, 128)), sds((TOK, 128)), sds((TOK, 128))], 9
    )(dq, dq_text, dk, dv, kv_got, from_low, from_high, back6, back2)
    home = exchanged(joined)
    image = kernel(spread_body, [sds((TOK, HEADS * 128))] * 3, 1)(home)
    return (*image, text_dq, text_dk, text_dv)


def solution(mesh):
    image = P(("outer", "inner"), None)
    text = P(None, "outer")
    share = P("inner", "outer")

    return jax.shard_map(
        shards,
        mesh=mesh,
        in_specs=(image,) * 6 + (text,) * 6,
        out_specs=(image,) * 3 + (share,) * 3,
        check_vma=False,
    )
```

profile of v0, /device:TPU:1, one launch (start us, length us, event | category | flops | bytes accessed | tf_op | source)
XLA Modules:
  0.0 96.2 jit_solution(13000561621846632487)
XLA Ops:
  0.6 2.9 %shard_map.163 = bf16[16,136,128]{2,1,0:T(8,128)(2,1)} custom-call(bf16[32,2048]{1,0:T(8,128)(2,1)} %q_in.1, bf16[32,2048]{1,0:T(8,128)(2,1)} %k_in.1, bf16[32,2048]{1,0:T(8,128)(2,1)} %v_in.1, bf16[32,2048]{1,0:T(8,128)(2,1)} %o_in.1, bf16[32,2048]{1,0:T(8,128)(2,1)} %g_in.1, f32[16,32]{1,0:T(8,128)} %bitcast.5), custom_call_target="tpu_custom_call" | custom-call | bytes 1048576 | tf_op jit(solution)/shard_map/pallas_call | solution.py:257
  3.6 17.9 %all_to_all.10.got = bf16[16,136,128]{2,1,0:T(8,128)(2,1)S(1)} all-to-all(bf16[16,136,128]{2,1,0:T(8,128)(2,1)} %shard_map.163), channel_id=1, replica_groups=mesh['outer'=16,'inner'=16] {'outer'}, dimensions={0} | all-to-all | bytes 1114112 | tf_op jit(solution)/shard_map/all_to_all | solution.py:252
  21.6 0.0 copy-start.5
  21.6 1.7 %collective-permute-start.1 = (bf16[1056,128]{1,0:T(8,128)(2,1)S(1)}, bf16[1056,128]{1,0:T(8,128)(2,1)S(1)}, u32[]{:S(2)}, u32[]{:S(2)}) collective-permute-start(bf16[1056,128]{1,0:T(8,128)(2,1)S(1)} %get-tuple-element.42.qg), channel_id=1, source_target_pairs={{0,2},{1,3},{2,4},{3,5},{4,6},{5,7},{6,8},{7,9},{8,10},{9,11},{10,... | collective-permute-start | bytes 811016 | tf_op jit(solution)/shard_map/ppermute | solution.py:249
  23.3 4.0 %collective-permute-start.3 = (bf16[1056,128]{1,0:T(8,128)(2,1)S(1)}, bf16[1056,128]{1,0:T(8,128)(2,1)S(1)}, u32[]{:S(2)}, u32[]{:S(2)}) collective-permute-start(bf16[1056,128]{1,0:T(8,128)(2,1)S(1)} %get-tuple-element.42.qg), channel_id=1, source_target_pairs={{0,14},{1,15},{2,0},{3,1},{4,2},{5,3},{6,4},{7,5},{8,6},{9,7},{10,... | collective-permute-start | bytes 811016 | tf_op jit(solution)/shard_map/ppermute | solution.py:249
  27.3 2.5 %collective-permute-start = (bf16[1024,128]{1,0:T(8,128)(2,1)S(1)}, bf16[1024,128]{1,0:T(8,128)(2,1)S(1)}, u32[]{:S(2)}, u32[]{:S(2)}) collective-permute-start(bf16[1024,128]{1,0:T(8,128)(2,1)S(1)} %get-tuple-element.39.kv_own), channel_id=1, source_target_pairs={{0,1},{1,0},{2,3},{3,2},{4,5},{5,4},{6,7},{7,6},{8,9},{9,8},{10,11... | collective-permute-start | bytes 786440 | tf_op jit(solution)/shard_map/ppermute | solution.py:255
  29.8 3.9 %collective-permute-done.1.refs_3_ = bf16[1056,128]{1,0:T(8,128)(2,1)S(1)} collective-permute-done((bf16[1056,128]{1,0:T(8,128)(2,1)S(1)}, bf16[1056,128]{1,0:T(8,128)(2,1)S(1)}, u32[]{:S(2)}, u32[]{:S(2)}) %collective-permute-start.1) | collective-permute-done | bytes 270368 | tf_op jit(solution)/shard_map/ppermute | solution.py:249
  33.7 0.0 collective-permute-start.2
  33.7 0.0 copy-done.5
  33.7 0.1 mul.22
  33.8 0.0 collective-permute-done.3.refs_4_
  33.8 2.7 %collective-permute-start.4 = (bf16[1056,128]{1,0:T(8,128)(2,1)S(1)}, bf16[1056,128]{1,0:T(8,128)(2,1)S(1)}, u32[]{:S(2)}, u32[]{:S(2)}) collective-permute-start(bf16[1056,128]{1,0:T(8,128)(2,1)S(1)} %collective-permute-done.3.refs_4_), channel_id=1, source_target_pairs={{0,14},{1,15},{2,0},{3,1},{4,2},{5,3},{6,4},{7,5},{8,6},{9,7},{10,... | collective-permute-start | bytes 811016 | tf_op jit(solution)/shard_map/ppermute | solution.py:249
  36.6 0.0 copy-done
  36.6 0.0 copy-done.4
  36.6 0.1 multiply_reduce_fusion
  36.7 0.1 stack.7
  36.9 0.1 reshape.32.text_ld
  36.9 5.0 %collective-permute-done.2.refs_3_ = bf16[1056,128]{1,0:T(8,128)(2,1)S(1)} collective-permute-done((bf16[1056,128]{1,0:T(8,128)(2,1)S(1)}, bf16[1056,128]{1,0:T(8,128)(2,1)S(1)}, u32[]{:S(2)}, u32[]{:S(2)}) %collective-permute-start.2) | collective-permute-done | bytes 270368 | tf_op jit(solution)/shard_map/ppermute | solution.py:249
  42.0 0.0 collective-permute-start.5
  42.0 0.0 collective-permute-done.kv_other
  42.0 0.0 copy-done.3
  42.0 1.0 shard_map.165
  43.0 0.0 collective-permute-done.4.refs_4_
  43.0 2.9 %collective-permute-start.7 = (bf16[1056,128]{1,0:T(8,128)(2,1)S(1)}, bf16[1056,128]{1,0:T(8,128)(2,1)S(1)}, u32[]{:S(2)}, u32[]{:S(2)}) collective-permute-start(bf16[1056,128]{1,0:T(8,128)(2,1)S(1)} %collective-permute-done.4.refs_4_), channel_id=1, source_target_pairs={{0,14},{1,15},{2,0},{3,1},{4,2},{5,3},{6,4},{7,5},{8,6},{9,7},{10,... | collective-permute-start | bytes 811016 | tf_op jit(solution)/shard_map/ppermute | solution.py:249
  45.9 3.3 %shard_map.166 = (bf16[544,128]{1,0:T(8,128)(2,1)S(1)}, bf16[544,128]{1,0:T(8,128)(2,1)S(1)}, f32[1088,128]{1,0:T(8,128)S(1)}, f32[1088,128]{1,0:T(8,128)S(1)}) custom-call(bf16[1088,128]{1,0:T(8,128)(2,1)S(1)} %get-tuple-element.40.refs_0_.keys, ...), custom_call_target="tpu_custom_call", output_to_operand_aliasing={{2}: (5, {}), {3}: (6, {})} | custom-call | flops 1426063360 | bytes 1048576 | tf_op jit(solution)/shard_map/pallas_call | solution.py:293
  49.3 3.3 %shard_map.167 = (f32[544,128]{1,0:T(8,128)S(1)}, f32[544,128]{1,0:T(8,128)S(1)}, f32[1088,128]{1,0:T(8,128)S(1)}, f32[1088,128]{1,0:T(8,128)S(1)}) custom-call(bf16[1088,128]{1,0:T(8,128)(2,1)S(1)} %get-tuple-element.40.refs_0_.keys, bf16[1088,128]{1,0:T(8,128)(2,1)S(1)} %get-tuple-element.41.refs_1_.values, ...), custom_call_target="tpu_custom_call", output_to_operand_aliasing={{2}: (5, {}), {3}: (6, {})} | custom-call | flops 1426063360 | bytes 1048576 | tf_op jit(solution)/shard_map/pallas_call | solution.py:293
  52.6 0.0 collective-permute-done.5.refs_3_
  52.6 0.1 collective-permute-start.6
  52.7 1.8 %shard_map.168 = (f32[512,128]{1,0:T(8,128)S(1)}, f32[1088,128]{1,0:T(8,128)S(1)}, f32[1088,128]{1,0:T(8,128)S(1)}) custom-call(bf16[1088,128]{1,0:T(8,128)(2,1)S(1)} %get-tuple-element.40.refs_0_.keys, bf16[1088,128]{1,0:T(8,128)(2,1)S(1)} %get-tuple-element.41.refs_1_.values, ...), custom_call_target="tpu_custom_call", output_to_operand_aliasing={{1}: (3, {}), {2}: (4, {})} | custom-call | flops 713031680 | bytes 1048576 | tf_op jit(solution)/shard_map/pallas_call | solution.py:303
  54.5 0.0 collective-permute-done.7.refs_4_
  54.5 3.3 %shard_map.169 = (bf16[1088,128]{1,0:T(8,128)(2,1)S(1)}, bf16[1088,128]{1,0:T(8,128)(2,1)S(1)}, f32[1088,128]{1,0:T(8,128)S(1)}, f32[1088,128]{1,0:T(8,128)S(1)}) custom-call(bf16[1088,128]{1,0:T(8,128)(2,1)S(1)} %get-tuple-element.40.refs_0_.keys, ...), custom_call_target="tpu_custom_call", output_to_operand_aliasing={{2}: (5, {}), {3}: (6, {})} | custom-call | flops 1426063360 | bytes 1048576 | tf_op jit(solution)/shard_map/pallas_call | solution.py:293
  57.8 0.3 collective-permute-start.9
  58.2 2.7 %collective-permute-start.10 = (bf16[1088,128]{1,0:T(8,128)(2,1)S(1)}, bf16[1088,128]{1,0:T(8,128)(2,1)S(1)}, u32[]{:S(2)}, u32[]{:S(2)}) collective-permute-start(bf16[1088,128]{1,0:T(8,128)(2,1)S(1)} %get-tuple-element.61), channel_id=1, source_target_pairs={{0,14},{1,15},{2,0},{3,1},{4,2},{5,3},{6,4},{7,5},{8,6},{9,7},{10,... | collective-permute-start | bytes 835592 | tf_op jit(solution)/shard_map/ppermute | solution.py:249
  60.9 0.0 collective-permute-done.6.refs_3_
  60.9 1.8 %shard_map.170 = (bf16[544,128]{1,0:T(8,128)(2,1)S(1)}, f32[1088,128]{1,0:T(8,128)S(1)}, f32[1088,128]{1,0:T(8,128)S(1)}, bf16[544,256]{1,0:T(8,128)(2,1)S(1)}) custom-call(bf16[1088,128]{1,0:T(8,128)(2,1)S(1)} %get-tuple-element.40.refs_0_.keys, ...), custom_call_target="tpu_custom_call", output_to_operand_aliasing={{1}: (4, {}), {2}: (5, {})} | custom-call | flops 713031680 | bytes 1048576 | tf_op jit(solution)/shard_map/pallas_call | solution.py:293
  62.7 1.2 %collective-permute-start.11 = (bf16[544,128]{1,0:T(8,128)(2,1)S(1)}, bf16[544,128]{1,0:T(8,128)(2,1)S(1)}, u32[]{:S(2)}, u32[]{:S(2)}) collective-permute-start(bf16[544,128]{1,0:T(8,128)(2,1)S(1)} %get-tuple-element.63), channel_id=1, source_target_pairs={{0,12},{1,13},{2,14},{3,15},{4,0},{5,1},{6,2},{7,3},{8,4},{9,5},{1... | collective-permute-start | bytes 417800 | tf_op jit(solution)/shard_map/ppermute | solution.py:249
  63.9 2.4 %collective-permute-start.8 = (bf16[544,256]{1,0:T(8,128)(2,1)S(1)}, bf16[544,256]{1,0:T(8,128)(2,1)S(1)}, u32[]{:S(2)}, u32[]{:S(2)}) collective-permute-start(bf16[544,256]{1,0:T(8,128)(2,1)S(1)} %get-tuple-element.59), channel_id=1, source_target_pairs={{0,1},{1,0},{2,3},{3,2},{4,5},{5,4},{6,7},{7,6},{8,9},{9,8},{10,11... | collective-permute-start | bytes 835592 | tf_op jit(solution)/shard_map/ppermute | solution.py:255
  66.3 0.0 collective-permute-done.9.refs_0_.from_low
  66.4 1.3 %collective-permute-start.13 = (bf16[544,128]{1,0:T(8,128)(2,1)S(1)}, bf16[544,128]{1,0:T(8,128)(2,1)S(1)}, u32[]{:S(2)}, u32[]{:S(2)}) collective-permute-start(bf16[544,128]{1,0:T(8,128)(2,1)S(1)} %shard_map.172), channel_id=1, source_target_pairs={{0,4},{1,5},{2,6},{3,7},{4,8},{5,9},{6,10},{7,11},{8,12},{9,13},{1... | collective-permute-start | bytes 417800 | tf_op jit(solution)/shard_map/ppermute | solution.py:249
  67.7 0.0 collective-permute-done.10.refs_0_.from_high
  67.7 2.2 %collective-permute-done.11.refs_1_ = bf16[544,128]{1,0:T(8,128)(2,1)S(1)} collective-permute-done((bf16[544,128]{1,0:T(8,128)(2,1)S(1)}, bf16[544,128]{1,0:T(8,128)(2,1)S(1)}, u32[]{:S(2)}, u32[]{:S(2)}) %collective-permute-start.11) | collective-permute-done | bytes 139296 | tf_op jit(solution)/shard_map/ppermute | solution.py:249
  70.0 2.4 %collective-permute-start.12 = (bf16[544,128]{1,0:T(8,128)(2,1)S(1)}, bf16[544,128]{1,0:T(8,128)(2,1)S(1)}, u32[]{:S(2)}, u32[]{:S(2)}) collective-permute-start(bf16[544,128]{1,0:T(8,128)(2,1)S(1)} %shard_map.171), channel_id=1, source_target_pairs={{0,12},{1,13},{2,14},{3,15},{4,0},{5,1},{6,2},{7,3},{8,4},{9,5},{1... | collective-permute-start | bytes 417800 | tf_op jit(solution)/shard_map/ppermute | solution.py:249
  72.4 1.5 %collective-permute-done.13.refs_1_ = bf16[544,128]{1,0:T(8,128)(2,1)S(1)} collective-permute-done((bf16[544,128]{1,0:T(8,128)(2,1)S(1)}, bf16[544,128]{1,0:T(8,128)(2,1)S(1)}, u32[]{:S(2)}, u32[]{:S(2)}) %collective-permute-start.13) | collective-permute-done | bytes 139296 | tf_op jit(solution)/shard_map/ppermute | solution.py:249
  73.9 4.4 %collective-permute-done.12.refs_0_ = bf16[544,128]{1,0:T(8,128)(2,1)S(1)} collective-permute-done((bf16[544,128]{1,0:T(8,128)(2,1)S(1)}, bf16[544,128]{1,0:T(8,128)(2,1)S(1)}, u32[]{:S(2)}, u32[]{:S(2)}) %collective-permute-start.12) | collective-permute-done | bytes 139296 | tf_op jit(solution)/shard_map/ppermute | solution.py:249
  78.2 0.0 collective-permute-done.8.kv_got
  78.2 0.6 shard_map.173
  78.9 16.5 %all_to_all.11.got = bf16[16,96,128]{2,1,0:T(8,128)(2,1)S(1)} all-to-all(bf16[16,96,128]{2,1,0:T(8,128)(2,1)S(1)} %get-tuple-element.65), channel_id=1, replica_groups=mesh['outer'=16,'inner'=16] {'outer'}, dimensions={0} | all-to-all | bytes 786432 | tf_op jit(solution)/shard_map/all_to_all | solution.py:252
  95.3 0.8 shard_map.174
  (13 shorter events, 0.2 us)
Async XLA Ops:
  21.5 15.1 %copy-start = (bf16[512,128]{1,0:T(8,128)(2,1)S(1)}, bf16[512,128]{1,0:T(8,128)(2,1)}, u32[]{:S(2)}) copy-start(bf16[512,128]{1,0:T(8,128)(2,1)} %text_g.1) | copy-start | bytes 393220
  21.5 15.1 %copy-start.4 = (bf16[512,128]{1,0:T(8,128)(2,1)S(1)}, bf16[512,128]{1,0:T(8,128)(2,1)}, u32[]{:S(2)}) copy-start(bf16[512,128]{1,0:T(8,128)(2,1)} %param.21) | copy-start | bytes 393220
  21.5 20.5 %copy-start.3 = (bf16[512,128]{1,0:T(8,128)(2,1)S(1)}, bf16[512,128]{1,0:T(8,128)(2,1)}, u32[]{:S(2)}) copy-start(bf16[512,128]{1,0:T(8,128)(2,1)} %text_q.1) | copy-start | bytes 393220
  21.6 12.1 %copy-start.5 = (f32[512,1]{0,1:T(1,128)S(1)}, f32[512,1]{0,1:T(1,128)}, u32[]{:S(2)}) copy-start(f32[512,1]{0,1:T(1,128)} %param.23) | copy-start | bytes 6148
  21.6 12.1 %collective-permute-start.1 = (bf16[1056,128]{1,0:T(8,128)(2,1)S(1)}, bf16[1056,128]{1,0:T(8,128)(2,1)S(1)}, u32[]{:S(2)}, u32[]{:S(2)}) collective-permute-start(bf16[1056,128]{1,0:T(8,128)(2,1)S(1)} %get-tuple-element.42.qg), channel_id=1, source_target_pairs={{0,2},{1,3},{2,4},{3,5},{4,6},{5,7},{6,8},{7,9},{8,10},{9,11},{10,... | collective-permute-start | bytes 811016 | tf_op jit(solution)/shard_map/ppermute | solution.py:249
  23.3 10.5 %collective-permute-start.3 = (bf16[1056,128]{1,0:T(8,128)(2,1)S(1)}, bf16[1056,128]{1,0:T(8,128)(2,1)S(1)}, u32[]{:S(2)}, u32[]{:S(2)}) collective-permute-start(bf16[1056,128]{1,0:T(8,128)(2,1)S(1)} %get-tuple-element.42.qg), channel_id=1, source_target_pairs={{0,14},{1,15},{2,0},{3,1},{4,2},{5,3},{6,4},{7,5},{8,6},{9,7},{10,... | collective-permute-start | bytes 811016 | tf_op jit(solution)/shard_map/ppermute | solution.py:249
  27.3 14.7 %collective-permute-start = (bf16[1024,128]{1,0:T(8,128)(2,1)S(1)}, bf16[1024,128]{1,0:T(8,128)(2,1)S(1)}, u32[]{:S(2)}, u32[]{:S(2)}) collective-permute-start(bf16[1024,128]{1,0:T(8,128)(2,1)S(1)} %get-tuple-element.39.kv_own), channel_id=1, source_target_pairs={{0,1},{1,0},{2,3},{3,2},{4,5},{5,4},{6,7},{7,6},{8,9},{9,8},{10,11... | collective-permute-start | bytes 786440 | tf_op jit(solution)/shard_map/ppermute | solution.py:255
  33.7 8.3 %collective-permute-start.2 = (bf16[1056,128]{1,0:T(8,128)(2,1)S(1)}, bf16[1056,128]{1,0:T(8,128)(2,1)S(1)}, u32[]{:S(2)}, u32[]{:S(2)}) collective-permute-start(bf16[1056,128]{1,0:T(8,128)(2,1)S(1)} %collective-permute-done.1.refs_3_), channel_id=1, source_target_pairs={{0,2},{1,3},{2,4},{3,5},{4,6},{5,7},{6,8},{7,9},{8,10},{9,11},{10,... | collective-permute-start | bytes 811016 | tf_op jit(solution)/shard_map/ppermute | solution.py:249
  33.8 8.2 %copy-start.1 = (bf16[512,128]{1,0:T(8,128)(2,1)S(1)}, bf16[512,128]{1,0:T(8,128)(2,1)}, u32[]{:S(2)}) copy-start(bf16[512,128]{1,0:T(8,128)(2,1)} %text_k.1) | copy-start | bytes 393220
  33.8 8.2 %copy-start.2 = (bf16[512,128]{1,0:T(8,128)(2,1)S(1)}, bf16[512,128]{1,0:T(8,128)(2,1)}, u32[]{:S(2)}) copy-start(bf16[512,128]{1,0:T(8,128)(2,1)} %text_v.1) | copy-start | bytes 393220
  33.8 9.1 %collective-permute-start.4 = (bf16[1056,128]{1,0:T(8,128)(2,1)S(1)}, bf16[1056,128]{1,0:T(8,128)(2,1)S(1)}, u32[]{:S(2)}, u32[]{:S(2)}) collective-permute-start(bf16[1056,128]{1,0:T(8,128)(2,1)S(1)} %collective-permute-done.3.refs_4_), channel_id=1, source_target_pairs={{0,14},{1,15},{2,0},{3,1},{4,2},{5,3},{6,4},{7,5},{8,6},{9,7},{10,... | collective-permute-start | bytes 811016 | tf_op jit(solution)/shard_map/ppermute | solution.py:249
  42.0 10.6 %collective-permute-start.5 = (bf16[1056,128]{1,0:T(8,128)(2,1)S(1)}, bf16[1056,128]{1,0:T(8,128)(2,1)S(1)}, u32[]{:S(2)}, u32[]{:S(2)}) collective-permute-start(bf16[1056,128]{1,0:T(8,128)(2,1)S(1)} %collective-permute-done.2.refs_3_), channel_id=1, source_target_pairs={{0,2},{1,3},{2,4},{3,5},{4,6},{5,7},{6,8},{7,9},{8,10},{9,11},{10,... | collective-permute-start | bytes 811016 | tf_op jit(solution)/shard_map/ppermute | solution.py:249
  43.0 11.5 %collective-permute-start.7 = (bf16[1056,128]{1,0:T(8,128)(2,1)S(1)}, bf16[1056,128]{1,0:T(8,128)(2,1)S(1)}, u32[]{:S(2)}, u32[]{:S(2)}) collective-permute-start(bf16[1056,128]{1,0:T(8,128)(2,1)S(1)} %collective-permute-done.4.refs_4_), channel_id=1, source_target_pairs={{0,14},{1,15},{2,0},{3,1},{4,2},{5,3},{6,4},{7,5},{8,6},{9,7},{10,... | collective-permute-start | bytes 811016 | tf_op jit(solution)/shard_map/ppermute | solution.py:249
  52.6 8.3 %collective-permute-start.6 = (bf16[1056,128]{1,0:T(8,128)(2,1)S(1)}, bf16[1056,128]{1,0:T(8,128)(2,1)S(1)}, u32[]{:S(2)}, u32[]{:S(2)}) collective-permute-start(bf16[1056,128]{1,0:T(8,128)(2,1)S(1)} %collective-permute-done.5.refs_3_), channel_id=1, source_target_pairs={{0,2},{1,3},{2,4},{3,5},{4,6},{5,7},{6,8},{7,9},{8,10},{9,11},{10,... | collective-permute-start | bytes 811016 | tf_op jit(solution)/shard_map/ppermute | solution.py:249
  57.8 8.5 %collective-permute-start.9 = (bf16[1088,128]{1,0:T(8,128)(2,1)S(1)}, bf16[1088,128]{1,0:T(8,128)(2,1)S(1)}, u32[]{:S(2)}, u32[]{:S(2)}) collective-permute-start(bf16[1088,128]{1,0:T(8,128)(2,1)S(1)} %get-tuple-element.60), channel_id=1, source_target_pairs={{0,2},{1,3},{2,4},{3,5},{4,6},{5,7},{6,8},{7,9},{8,10},{9,11},{10,... | collective-permute-start | bytes 835592 | tf_op jit(solution)/shard_map/ppermute | solution.py:249
  58.2 9.6 %collective-permute-start.10 = (bf16[1088,128]{1,0:T(8,128)(2,1)S(1)}, bf16[1088,128]{1,0:T(8,128)(2,1)S(1)}, u32[]{:S(2)}, u32[]{:S(2)}) collective-permute-start(bf16[1088,128]{1,0:T(8,128)(2,1)S(1)} %get-tuple-element.61), channel_id=1, source_target_pairs={{0,14},{1,15},{2,0},{3,1},{4,2},{5,3},{6,4},{7,5},{8,6},{9,7},{10,... | collective-permute-start | bytes 835592 | tf_op jit(solution)/shard_map/ppermute | solution.py:249
  62.7 7.2 %collective-permute-start.11 = (bf16[544,128]{1,0:T(8,128)(2,1)S(1)}, bf16[544,128]{1,0:T(8,128)(2,1)S(1)}, u32[]{:S(2)}, u32[]{:S(2)}) collective-permute-start(bf16[544,128]{1,0:T(8,128)(2,1)S(1)} %get-tuple-element.63), channel_id=1, source_target_pairs={{0,12},{1,13},{2,14},{3,15},{4,0},{5,1},{6,2},{7,3},{8,4},{9,5},{1... | collective-permute-start | bytes 417800 | tf_op jit(solution)/shard_map/ppermute | solution.py:249
  63.9 14.3 %collective-permute-start.8 = (bf16[544,256]{1,0:T(8,128)(2,1)S(1)}, bf16[544,256]{1,0:T(8,128)(2,1)S(1)}, u32[]{:S(2)}, u32[]{:S(2)}) collective-permute-start(bf16[544,256]{1,0:T(8,128)(2,1)S(1)} %get-tuple-element.59), channel_id=1, source_target_pairs={{0,1},{1,0},{2,3},{3,2},{4,5},{5,4},{6,7},{7,6},{8,9},{9,8},{10,11... | collective-permute-start | bytes 835592 | tf_op jit(solution)/shard_map/ppermute | solution.py:255
  66.4 7.5 %collective-permute-start.13 = (bf16[544,128]{1,0:T(8,128)(2,1)S(1)}, bf16[544,128]{1,0:T(8,128)(2,1)S(1)}, u32[]{:S(2)}, u32[]{:S(2)}) collective-permute-start(bf16[544,128]{1,0:T(8,128)(2,1)S(1)} %shard_map.172), channel_id=1, source_target_pairs={{0,4},{1,5},{2,6},{3,7},{4,8},{5,9},{6,10},{7,11},{8,12},{9,13},{1... | collective-permute-start | bytes 417800 | tf_op jit(solution)/shard_map/ppermute | solution.py:249
  70.0 8.2 %collective-permute-start.12 = (bf16[544,128]{1,0:T(8,128)(2,1)S(1)}, bf16[544,128]{1,0:T(8,128)(2,1)S(1)}, u32[]{:S(2)}, u32[]{:S(2)}) collective-permute-start(bf16[544,128]{1,0:T(8,128)(2,1)S(1)} %shard_map.171), channel_id=1, source_target_pairs={{0,12},{1,13},{2,14},{3,15},{4,0},{5,1},{6,2},{7,3},{8,4},{9,5},{1... | collective-permute-start | bytes 417800 | tf_op jit(solution)/shard_map/ppermute | solution.py:249
where the time goes:
time: 96.4 us; the launch traced here: 96.2 us
  blocking collectives  34.4 us (36%)
  starting transfers between devices  24.4 us (25%)
  Pallas kernels  19.1 us (20%)
  waiting for transfers between devices  17 us (18%)
    all_to_all x2, blocking collectives, exchanged(): return lax.all_to_all(x, 'outer', split_axis=0, concat_axis=0, tiled=True)  34.4 us
    ppermute x12, starting transfers between devices, along_ring(): return lax.ppermute(x, 'inner', pairs)  19.5 us
    ppermute x12, waiting for transfers between devices, along_ring(): return lax.ppermute(x, 'inner', pairs)  17 us
    pallas_call x4, Pallas kernels, shards(): kernel(functools.partial(far_body, step), [part] * count + [acc, acc] + (...  11.8 us
    ppermute x2, starting transfers between devices, across(): return lax.ppermute(x, 'inner', [(n, n ^ 1) for n in range(2 * RING)])  4.89 us
    pallas_call x1, Pallas kernels, shards(): kernel(pack_body, sds((HEADS, CHUNK, 128)), [HB] * 5 + [VM], scratch=[plt...  2.95 us
  transfers between devices with their start and end apart: 14, of which 5 were waited for; matrix products, arithmetic and copies ran while one was open for 0% of the time, Pallas kernels for 15%

commit v1 on v0

--- a/solution.py
+++ b/solution.py
@@ -137,39 +137,32 @@
     dq_text[...] = one_block(tq[...], tg[...], logs, deltas, keys, values, dk, dv).astype(BF16)
 
 
-def own_body(keys, values, qg, dk_in, dv_in, dq, dk, dv):
+def own_body(keys, values, qg, dk_in, dv_in, dq, dk, dv, send):
+    _, side = place()
     dk[...] = dk_in[...]
     dv[...] = dv_in[...]
     q, g, logs, deltas = block_operands(qg)
     dq[...] = one_block(q, g, logs, deltas, keys, values, dk, dv)
-
-
-def far_body(step, *refs):
-    keys, values, dq_text = refs[:3]
-    z, side = place()
-    count = 2 if step < 4 else 1
-    blocks, refs = refs[3 : 3 + count], refs[3 + count :]
-    (dk_in, dv_in), refs = refs[:2], refs[2:]
-    if step == 3:
-        firsts, refs = refs[:2], refs[2:]
-    dqs, refs = refs[:count], refs[count:]
-    (dk, dv), refs = refs[:2], refs[2:]
+    text = pl.ds(pl.multiple_of(2 * NEAR + (1 - side) * TOK, TOK), TOK)
+    for source, lanes, factor in ((dk, slice(0, 128), SCALE), (dv, slice(128, 256), 1.0)):
+        send[0:NEAR, lanes] = (source[NEAR : 2 * NEAR, :] * factor).astype(BF16)
+        send[NEAR:OWN, lanes] = (source[text, :] * factor).astype(BF16)
+
+
+def far_body(step, offset, *refs):
+    keys, values, dq_text, qg, dk_in, dv_in = refs[:6]
+    first, refs = (refs[6], refs[7:]) if step == 3 else (None, refs[6:])
+    dq, dk, dv = refs[:3]
+    z, _ = place()
     dk[...] = dk_in[...]
     dv[...] = dv_in[...]
-    for n, (qg, dq) in enumerate(zip(blocks, dqs)):
-        q, g, logs, deltas = block_operands(qg)
-        dq[0:NEAR, :] = one_block(q, g, logs, deltas, keys, values, dk, dv).astype(dq.dtype)
-        owner = lax.rem(z + (step if n == 1 else RING - step), RING)
-        text = dq_text[pl.ds(pl.multiple_of(owner * TOK, TOK), TOK), :]
-        dq[NEAR:OWN, :] = text.astype(dq.dtype)
-        if step == 3:
-            dq[OWN : 2 * OWN, :] = firsts[n][...]
-    if step == 4:
-        (send,) = refs
-        text = pl.ds(pl.multiple_of(2 * NEAR + (1 - side) * TOK, TOK), TOK)
-        for source, lanes, factor in ((dk, slice(0, 128), SCALE), (dv, slice(128, 256), 1.0)):
-            send[0:NEAR, lanes] = (source[NEAR : 2 * NEAR, :] * factor).astype(BF16)
-            send[NEAR:OWN, lanes] = (source[text, :] * factor).astype(BF16)
+    q, g, logs, deltas = block_operands(qg)
+    dq[0:NEAR, :] = one_block(q, g, logs, deltas, keys, values, dk, dv).astype(dq.dtype)
+    owner = lax.rem(z + offset, RING)
+    text = dq_text[pl.ds(pl.multiple_of(owner * TOK, TOK), TOK), :]
+    dq[NEAR:OWN, :] = text.astype(dq.dtype)
+    if step == 3:
+        dq[OWN : 2 * OWN, :] = first[...]
 
 
 def mid_body(mine, *refs):
@@ -283,27 +276,25 @@
     up = down = qg
     parts = {}
     for step in range(1, 5):
+        part = {1: sds((OWN, 128)), 2: sds((OWN, 128), F32), 3: sds((2 * OWN, 128)), 4: sds((OWN, 128))}[step]
+        parts[step] = []
         up = along_ring(up, 1)
-        blocks = [up]
         if step < 4:
             down = along_ring(down, -1)
-            blocks.append(down)
-        count = len(blocks)
-        part = {1: sds((OWN, 128)), 2: sds((OWN, 128), F32), 3: sds((2 * OWN, 128)), 4: sds((OWN, 128))}[step]
-        result = kernel(
-            functools.partial(far_body, step),
-            [part] * count + [acc, acc] + ([sds((OWN, 256))] if step == 4 else []),
-            5 + count + (2 if step == 3 else 0),
-            flops=block_flops(NEAR * count),
-            aliases={3 + count: count, 4 + count: count + 1},
-        )(keys, values, dq_text, *blocks, dk, dv, *(parts[1] if step == 3 else ()))
-        parts[step] = result[:count]
-        dk, dv = result[count : count + 2]
-        if step == 2:
-            dq, dk, dv = kernel(
-                own_body, [sds((NEAR, 128), F32), acc, acc], 5, flops=block_flops(NEAR), aliases={3: 1, 4: 2}
-            )(keys, values, qg, dk, dv)
-    kv_got = across(result[-1])
+        for n, moved in enumerate((up, down) if step < 4 else (up,)):
+            result = kernel(
+                functools.partial(far_body, step, step if n else RING - step),
+                [part, acc, acc],
+                7 if step == 3 else 6,
+                flops=block_flops(NEAR),
+                aliases={4: 1, 5: 2},
+            )(keys, values, dq_text, moved, dk, dv, *(parts[1][n : n + 1] if step == 3 else ()))
+            parts[step].append(result[0])
+            dk, dv = result[1:3]
+    dq, dk, dv, send = kernel(
+        own_body, [sds((NEAR, 128), F32), acc, acc, sds((OWN, 256))], 5, flops=block_flops(NEAR), aliases={3: 1, 4: 2}
+    )(keys, values, qg, dk, dv)
+    kv_got = across(send)
     from_high = along_ring(parts[3][0], -1)
     from_low = along_ring(parts[3][1], 1)
     from_far = along_ring(parts[4][0], -2)

time: 96.4 us -> 96.2 us (level)
    pallas_call x5 -> x8, Pallas kernels: 13.6 us -> 14.3 us  [the longest x7 12.5 us: shards(): kernel(functools.partial(far_body, step, step if n else RING - step), [pa...]
  transfers between devices with their start and end apart: 14 -> 14, of which waited for: 5 -> 6; matrix products, arithmetic and copies ran while one was open for 0% -> 0% of each run, Pallas kernels for 15% -> 16%
where the time goes in v1:
time: 96.2 us; the launch traced here: 95.9 us
  blocking collectives  34.2 us (36%)
  starting transfers between devices  23.8 us (25%)
  Pallas kernels  19.8 us (21%)
  waiting for transfers between devices  16.9 us (18%)
    all_to_all x2, blocking collectives, exchanged(): return lax.all_to_all(x, 'outer', split_axis=0, concat_axis=0, tiled=True)  34.2 us
    ppermute x12, starting transfers between devices, along_ring(): return lax.ppermute(x, 'inner', pairs)  19.8 us
    ppermute x12, waiting for transfers between devices, along_ring(): return lax.ppermute(x, 'inner', pairs)  16.9 us
    pallas_call x7, Pallas kernels, shards(): kernel(functools.partial(far_body, step, step if n else RING - step), [pa...  12.5 us
    ppermute x2, starting transfers between devices, across(): return lax.ppermute(x, 'inner', [(n, n ^ 1) for n in range(2 * RING)])  4.05 us
    pallas_call x1, Pallas kernels, shards(): kernel(pack_body, sds((HEADS, CHUNK, 128)), [HB] * 5 + [VM], scratch=[plt...  2.95 us
  transfers between devices with their start and end apart: 14, of which 6 were waited for; matrix products, arithmetic and copies ran while one was open for 0% of the time, Pallas kernels for 16%

profile of v1, /device:TPU:1, one launch (start us, length us, event | category | flops | bytes accessed | tf_op | source)
XLA Modules:
  0.0 95.9 jit_solution(10293577611789532812)
XLA Ops:
  0.6 3.0 %shard_map.163 = bf16[16,136,128]{2,1,0:T(8,128)(2,1)} custom-call(bf16[32,2048]{1,0:T(8,128)(2,1)} %q_in.1, bf16[32,2048]{1,0:T(8,128)(2,1)} %k_in.1, bf16[32,2048]{1,0:T(8,128)(2,1)} %v_in.1, bf16[32,2048]{1,0:T(8,128)(2,1)} %o_in.1, bf16[32,2048]{1,0:T(8,128)(2,1)} %g_in.1, f32[16,32]{1,0:T(8,128)} %bitcast.5), custom_call_target="tpu_custom_call" | custom-call | bytes 1048576 | tf_op jit(solution)/shard_map/pallas_call | solution.py:250
  3.6 17.9 %all_to_all.10.got = bf16[16,136,128]{2,1,0:T(8,128)(2,1)S(1)} all-to-all(bf16[16,136,128]{2,1,0:T(8,128)(2,1)} %shard_map.163), channel_id=1, replica_groups=mesh['outer'=16,'inner'=16] {'outer'}, dimensions={0} | all-to-all | bytes 1114112 | tf_op jit(solution)/shard_map/all_to_all | solution.py:245
  21.6 0.0 copy-start.5
  21.6 1.7 %collective-permute-start.1 = (bf16[1056,128]{1,0:T(8,128)(2,1)S(1)}, bf16[1056,128]{1,0:T(8,128)(2,1)S(1)}, u32[]{:S(2)}, u32[]{:S(2)}) collective-permute-start(bf16[1056,128]{1,0:T(8,128)(2,1)S(1)} %get-tuple-element.48.qg), channel_id=1, source_target_pairs={{0,2},{1,3},{2,4},{3,5},{4,6},{5,7},{6,8},{7,9},{8,10},{9,11},{10,... | collective-permute-start | bytes 811016 | tf_op jit(solution)/shard_map/ppermute | solution.py:242
  23.3 4.0 %collective-permute-start.5 = (bf16[1056,128]{1,0:T(8,128)(2,1)S(1)}, bf16[1056,128]{1,0:T(8,128)(2,1)S(1)}, u32[]{:S(2)}, u32[]{:S(2)}) collective-permute-start(bf16[1056,128]{1,0:T(8,128)(2,1)S(1)} %get-tuple-element.48.qg), channel_id=1, source_target_pairs={{0,14},{1,15},{2,0},{3,1},{4,2},{5,3},{6,4},{7,5},{8,6},{9,7},{10,... | collective-permute-start | bytes 811016 | tf_op jit(solution)/shard_map/ppermute | solution.py:242
  27.3 6.4 %collective-permute-done.1.refs_3_ = bf16[1056,128]{1,0:T(8,128)(2,1)S(1)} collective-permute-done((bf16[1056,128]{1,0:T(8,128)(2,1)S(1)}, bf16[1056,128]{1,0:T(8,128)(2,1)S(1)}, u32[]{:S(2)}, u32[]{:S(2)}) %collective-permute-start.1) | collective-permute-done | bytes 270368 | tf_op jit(solution)/shard_map/ppermute | solution.py:242
  33.7 0.0 collective-permute-start.2
  33.7 2.5 %collective-permute-start = (bf16[1024,128]{1,0:T(8,128)(2,1)S(1)}, bf16[1024,128]{1,0:T(8,128)(2,1)S(1)}, u32[]{:S(2)}, u32[]{:S(2)}) collective-permute-start(bf16[1024,128]{1,0:T(8,128)(2,1)S(1)} %get-tuple-element.45.kv_own), channel_id=1, source_target_pairs={{0,1},{1,0},{2,3},{3,2},{4,5},{5,4},{6,7},{7,6},{8,9},{9,8},{10,11... | collective-permute-start | bytes 786440 | tf_op jit(solution)/shard_map/ppermute | solution.py:248
  36.2 0.1 mul.22
  36.3 0.0 collective-permute-done.5.refs_3_
  36.3 2.7 %collective-permute-start.6 = (bf16[1056,128]{1,0:T(8,128)(2,1)S(1)}, bf16[1056,128]{1,0:T(8,128)(2,1)S(1)}, u32[]{:S(2)}, u32[]{:S(2)}) collective-permute-start(bf16[1056,128]{1,0:T(8,128)(2,1)S(1)} %collective-permute-done.5.refs_3_), channel_id=1, source_target_pairs={{0,14},{1,15},{2,0},{3,1},{4,2},{5,3},{6,4},{7,5},{8,6},{9,7},{10,... | collective-permute-start | bytes 811016 | tf_op jit(solution)/shard_map/ppermute | solution.py:242
  39.0 0.1 multiply_reduce_fusion
  39.2 0.1 stack.7
  39.3 2.7 %collective-permute-done.2.refs_3_ = bf16[1056,128]{1,0:T(8,128)(2,1)S(1)} collective-permute-done((bf16[1056,128]{1,0:T(8,128)(2,1)S(1)}, bf16[1056,128]{1,0:T(8,128)(2,1)S(1)}, u32[]{:S(2)}, u32[]{:S(2)}) %collective-permute-start.2) | collective-permute-done | bytes 270368 | tf_op jit(solution)/shard_map/ppermute | solution.py:242
  42.0 0.0 collective-permute-start.3
  42.0 0.1 reshape.32.text_ld
  42.1 0.0 collective-permute-done.kv_other
  42.1 0.9 shard_map.165
  43.1 0.3 collective-permute-done.6.refs_3_
  43.3 3.4 %collective-permute-start.7 = (bf16[1056,128]{1,0:T(8,128)(2,1)S(1)}, bf16[1056,128]{1,0:T(8,128)(2,1)S(1)}, u32[]{:S(2)}, u32[]{:S(2)}) collective-permute-start(bf16[1056,128]{1,0:T(8,128)(2,1)S(1)} %collective-permute-done.6.refs_3_), channel_id=1, source_target_pairs={{0,14},{1,15},{2,0},{3,1},{4,2},{5,3},{6,4},{7,5},{8,6},{9,7},{10,... | collective-permute-start | bytes 811016 | tf_op jit(solution)/shard_map/ppermute | solution.py:242
  46.8 1.8 %shard_map.166 = (bf16[544,128]{1,0:T(8,128)(2,1)S(1)}, f32[1088,128]{1,0:T(8,128)S(1)}, f32[1088,128]{1,0:T(8,128)S(1)}) custom-call(bf16[1088,128]{1,0:T(8,128)(2,1)S(1)} %get-tuple-element.46.refs_0_.keys, bf16[1088,128]{1,0:T(8,128)(2,1)S(1)} %get-tuple-element.47.refs_1_.values, ...), custom_call_target="tpu_custom_call", output_to_operand_aliasing={{1}: (4, {}), {2}: (5, {})} | custom-call | flops 713031680 | bytes 1048576 | tf_op jit(solution)/shard_map/pallas_call | solution.py:285
  48.6 1.8 %shard_map.167 = (bf16[544,128]{1,0:T(8,128)(2,1)S(1)}, f32[1088,128]{1,0:T(8,128)S(1)}, f32[1088,128]{1,0:T(8,128)S(1)}) custom-call(bf16[1088,128]{1,0:T(8,128)(2,1)S(1)} %get-tuple-element.46.refs_0_.keys, bf16[1088,128]{1,0:T(8,128)(2,1)S(1)} %get-tuple-element.47.refs_1_.values, ...), custom_call_target="tpu_custom_call", output_to_operand_aliasing={{1}: (4, {}), {2}: (5, {})} | custom-call | flops 713031680 | bytes 1048576 | tf_op jit(solution)/shard_map/pallas_call | solution.py:285
  50.3 0.0 collective-permute-done.3.refs_3_
  50.4 0.3 collective-permute-start.4
  50.6 1.8 %shard_map.168 = (f32[544,128]{1,0:T(8,128)S(1)}, f32[1088,128]{1,0:T(8,128)S(1)}, f32[1088,128]{1,0:T(8,128)S(1)}) custom-call(bf16[1088,128]{1,0:T(8,128)(2,1)S(1)} %get-tuple-element.46.refs_0_.keys, bf16[1088,128]{1,0:T(8,128)(2,1)S(1)} %get-tuple-element.47.refs_1_.values, ...), custom_call_target="tpu_custom_call", output_to_operand_aliasing={{1}: (4, {}), {2}: (5, {})} | custom-call | flops 713031680 | bytes 1048576 | tf_op jit(solution)/shard_map/pallas_call | solution.py:285
  52.4 1.8 %shard_map.169 = (f32[544,128]{1,0:T(8,128)S(1)}, f32[1088,128]{1,0:T(8,128)S(1)}, f32[1088,128]{1,0:T(8,128)S(1)}) custom-call(bf16[1088,128]{1,0:T(8,128)(2,1)S(1)} %get-tuple-element.46.refs_0_.keys, bf16[1088,128]{1,0:T(8,128)(2,1)S(1)} %get-tuple-element.47.refs_1_.values, ...), custom_call_target="tpu_custom_call", output_to_operand_aliasing={{1}: (4, {}), {2}: (5, {})} | custom-call | flops 713031680 | bytes 1048576 | tf_op jit(solution)/shard_map/pallas_call | solution.py:285
  54.2 1.8 %shard_map.170 = (bf16[1088,128]{1,0:T(8,128)(2,1)S(1)}, f32[1088,128]{1,0:T(8,128)S(1)}, f32[1088,128]{1,0:T(8,128)S(1)}) custom-call(bf16[1088,128]{1,0:T(8,128)(2,1)S(1)} %get-tuple-element.46.refs_0_.keys, bf16[1088,128]{1,0:T(8,128)(2,1)S(1)} %get-tuple-element.47.refs_1_.values, ...), custom_call_target="tpu_custom_call", output_to_operand_aliasing={{1}: (4, {}), {2}: (5, {})} | custom-call | flops 713031680 | bytes 1048576 | tf_op jit(solution)/shard_map/pallas_call | solution.py:285
  56.0 0.0 collective-permute-done.7.refs_3_
  56.0 1.8 %shard_map.171 = (bf16[1088,128]{1,0:T(8,128)(2,1)S(1)}, f32[1088,128]{1,0:T(8,128)S(1)}, f32[1088,128]{1,0:T(8,128)S(1)}) custom-call(bf16[1088,128]{1,0:T(8,128)(2,1)S(1)} %get-tuple-element.46.refs_0_.keys, bf16[1088,128]{1,0:T(8,128)(2,1)S(1)} %get-tuple-element.47.refs_1_.values, ...), custom_call_target="tpu_custom_call", output_to_operand_aliasing={{1}: (4, {}), {2}: (5, {})} | custom-call | flops 713031680 | bytes 1048576 | tf_op jit(solution)/shard_map/pallas_call | solution.py:285
  57.8 0.1 collective-permute-start.9
  57.9 2.7 %collective-permute-start.10 = (bf16[1088,128]{1,0:T(8,128)(2,1)S(1)}, bf16[1088,128]{1,0:T(8,128)(2,1)S(1)}, u32[]{:S(2)}, u32[]{:S(2)}) collective-permute-start(bf16[1088,128]{1,0:T(8,128)(2,1)S(1)} %get-tuple-element.73), channel_id=1, source_target_pairs={{0,14},{1,15},{2,0},{3,1},{4,2},{5,3},{6,4},{7,5},{8,6},{9,7},{10,... | collective-permute-start | bytes 835592 | tf_op jit(solution)/shard_map/ppermute | solution.py:242
  60.6 0.0 collective-permute-done.4.refs_3_
  60.6 1.8 %shard_map.172 = (bf16[544,128]{1,0:T(8,128)(2,1)S(1)}, f32[1088,128]{1,0:T(8,128)S(1)}, f32[1088,128]{1,0:T(8,128)S(1)}) custom-call(bf16[1088,128]{1,0:T(8,128)(2,1)S(1)} %get-tuple-element.46.refs_0_.keys, bf16[1088,128]{1,0:T(8,128)(2,1)S(1)} %get-tuple-element.47.refs_1_.values, ...), custom_call_target="tpu_custom_call", output_to_operand_aliasing={{1}: (4, {}), {2}: (5, {})} | custom-call | flops 713031680 | bytes 1048576 | tf_op jit(solution)/shard_map/pallas_call | solution.py:285
  62.4 1.4 %collective-permute-start.11 = (bf16[544,128]{1,0:T(8,128)(2,1)S(1)}, bf16[544,128]{1,0:T(8,128)(2,1)S(1)}, u32[]{:S(2)}, u32[]{:S(2)}) collective-permute-start(bf16[544,128]{1,0:T(8,128)(2,1)S(1)} %get-tuple-element.75), channel_id=1, source_target_pairs={{0,12},{1,13},{2,14},{3,15},{4,0},{5,1},{6,2},{7,3},{8,4},{9,5},{1... | collective-permute-start | bytes 417800 | tf_op jit(solution)/shard_map/ppermute | solution.py:242
  63.8 1.8 %shard_map.173 = (f32[512,128]{1,0:T(8,128)S(1)}, f32[1088,128]{1,0:T(8,128)S(1)}, f32[1088,128]{1,0:T(8,128)S(1)}, bf16[544,256]{1,0:T(8,128)(2,1)S(1)}) custom-call(bf16[1088,128]{1,0:T(8,128)(2,1)S(1)} %get-tuple-element.46.refs_0_.keys, bf16[1088,128]{1,0:T(8,128)(2,1)S(1)} %get-tuple-element.47.refs_1_.values, ...), custom_call_target="tpu_custom_call", output_to_operand_aliasing={{1}: (3, {}), {2}: (4, {})} | custom-call | flops 713031680 | bytes 1048576 | tf_op jit(solution)/shard_map/pallas_call | solution.py:294
  65.6 1.6 %collective-permute-start.8 = (bf16[544,256]{1,0:T(8,128)(2,1)S(1)}, bf16[544,256]{1,0:T(8,128)(2,1)S(1)}, u32[]{:S(2)}, u32[]{:S(2)}) collective-permute-start(bf16[544,256]{1,0:T(8,128)(2,1)S(1)} %get-tuple-element.71), channel_id=1, source_target_pairs={{0,1},{1,0},{2,3},{3,2},{4,5},{5,4},{6,7},{7,6},{8,9},{9,8},{10,11... | collective-permute-start | bytes 835592 | tf_op jit(solution)/shard_map/ppermute | solution.py:248
  67.2 0.0 collective-permute-done.9.refs_0_.from_low
  67.3 1.3 %collective-permute-start.13 = (bf16[544,128]{1,0:T(8,128)(2,1)S(1)}, bf16[544,128]{1,0:T(8,128)(2,1)S(1)}, u32[]{:S(2)}, u32[]{:S(2)}) collective-permute-start(bf16[544,128]{1,0:T(8,128)(2,1)S(1)} %shard_map.175), channel_id=1, source_target_pairs={{0,4},{1,5},{2,6},{3,7},{4,8},{5,9},{6,10},{7,11},{8,12},{9,13},{1... | collective-permute-start | bytes 417800 | tf_op jit(solution)/shard_map/ppermute | solution.py:242
  68.6 0.0 collective-permute-done.10.refs_0_.from_high
  68.6 1.4 %collective-permute-done.11.refs_1_ = bf16[544,128]{1,0:T(8,128)(2,1)S(1)} collective-permute-done((bf16[544,128]{1,0:T(8,128)(2,1)S(1)}, bf16[544,128]{1,0:T(8,128)(2,1)S(1)}, u32[]{:S(2)}, u32[]{:S(2)}) %collective-permute-start.11) | collective-permute-done | bytes 139296 | tf_op jit(solution)/shard_map/ppermute | solution.py:242
  70.0 0.1 shard_map.174
  70.0 2.0 %collective-permute-start.12 = (bf16[544,128]{1,0:T(8,128)(2,1)S(1)}, bf16[544,128]{1,0:T(8,128)(2,1)S(1)}, u32[]{:S(2)}, u32[]{:S(2)}) collective-permute-start(bf16[544,128]{1,0:T(8,128)(2,1)S(1)} %shard_map.174), channel_id=1, source_target_pairs={{0,12},{1,13},{2,14},{3,15},{4,0},{5,1},{6,2},{7,3},{8,4},{9,5},{1... | collective-permute-start | bytes 417800 | tf_op jit(solution)/shard_map/ppermute | solution.py:242
  72.1 2.7 %collective-permute-done.13.refs_1_ = bf16[544,128]{1,0:T(8,128)(2,1)S(1)} collective-permute-done((bf16[544,128]{1,0:T(8,128)(2,1)S(1)}, bf16[544,128]{1,0:T(8,128)(2,1)S(1)}, u32[]{:S(2)}, u32[]{:S(2)}) %collective-permute-start.13) | collective-permute-done | bytes 139296 | tf_op jit(solution)/shard_map/ppermute | solution.py:242
  74.8 3.4 %collective-permute-done.12.refs_0_ = bf16[544,128]{1,0:T(8,128)(2,1)S(1)} collective-permute-done((bf16[544,128]{1,0:T(8,128)(2,1)S(1)}, bf16[544,128]{1,0:T(8,128)(2,1)S(1)}, u32[]{:S(2)}, u32[]{:S(2)}) %collective-permute-start.12) | collective-permute-done | bytes 139296 | tf_op jit(solution)/shard_map/ppermute | solution.py:242
  78.2 0.0 collective-permute-done.8.kv_got
  78.2 0.6 shard_map.176
  78.8 16.2 %all_to_all.11.got = bf16[16,96,128]{2,1,0:T(8,128)(2,1)S(1)} all-to-all(bf16[16,96,128]{2,1,0:T(8,128)(2,1)S(1)} %get-tuple-element.77), channel_id=1, replica_groups=mesh['outer'=16,'inner'=16] {'outer'}, dimensions={0} | all-to-all | bytes 786432 | tf_op jit(solution)/shard_map/all_to_all | solution.py:245
  95.1 0.8 shard_map.177
  (16 shorter events, 0.1 us)
Async XLA Ops:
  21.5 17.5 %copy-start = (bf16[512,128]{1,0:T(8,128)(2,1)S(1)}, bf16[512,128]{1,0:T(8,128)(2,1)}, u32[]{:S(2)}) copy-start(bf16[512,128]{1,0:T(8,128)(2,1)} %text_g.1) | copy-start | bytes 393220
  21.5 17.5 %copy-start.4 = (bf16[512,128]{1,0:T(8,128)(2,1)S(1)}, bf16[512,128]{1,0:T(8,128)(2,1)}, u32[]{:S(2)}) copy-start(bf16[512,128]{1,0:T(8,128)(2,1)} %param.21) | copy-start | bytes 393220
  21.5 20.6 %copy-start.3 = (bf16[512,128]{1,0:T(8,128)(2,1)S(1)}, bf16[512,128]{1,0:T(8,128)(2,1)}, u32[]{:S(2)}) copy-start(bf16[512,128]{1,0:T(8,128)(2,1)} %text_q.1) | copy-start | bytes 393220
  21.6 14.6 %copy-start.5 = (f32[512,1]{0,1:T(1,128)S(1)}, f32[512,1]{0,1:T(1,128)}, u32[]{:S(2)}) copy-start(f32[512,1]{0,1:T(1,128)} %param.23) | copy-start | bytes 6148
  21.6 12.1 %collective-permute-start.1 = (bf16[1056,128]{1,0:T(8,128)(2,1)S(1)}, bf16[1056,128]{1,0:T(8,128)(2,1)S(1)}, u32[]{:S(2)}, u32[]{:S(2)}) collective-permute-start(bf16[1056,128]{1,0:T(8,128)(2,1)S(1)} %get-tuple-element.48.qg), channel_id=1, source_target_pairs={{0,2},{1,3},{2,4},{3,5},{4,6},{5,7},{6,8},{7,9},{8,10},{9,11},{10,... | collective-permute-start | bytes 811016 | tf_op jit(solution)/shard_map/ppermute | solution.py:242
  23.3 13.0 %collective-permute-start.5 = (bf16[1056,128]{1,0:T(8,128)(2,1)S(1)}, bf16[1056,128]{1,0:T(8,128)(2,1)S(1)}, u32[]{:S(2)}, u32[]{:S(2)}) collective-permute-start(bf16[1056,128]{1,0:T(8,128)(2,1)S(1)} %get-tuple-element.48.qg), channel_id=1, source_target_pairs={{0,14},{1,15},{2,0},{3,1},{4,2},{5,3},{6,4},{7,5},{8,6},{9,7},{10,... | collective-permute-start | bytes 811016 | tf_op jit(solution)/shard_map/ppermute | solution.py:242
  33.7 8.3 %collective-permute-start.2 = (bf16[1056,128]{1,0:T(8,128)(2,1)S(1)}, bf16[1056,128]{1,0:T(8,128)(2,1)S(1)}, u32[]{:S(2)}, u32[]{:S(2)}) collective-permute-start(bf16[1056,128]{1,0:T(8,128)(2,1)S(1)} %collective-permute-done.1.refs_3_), channel_id=1, source_target_pairs={{0,2},{1,3},{2,4},{3,5},{4,6},{5,7},{6,8},{7,9},{8,10},{9,11},{10,... | collective-permute-start | bytes 811016 | tf_op jit(solution)/shard_map/ppermute | solution.py:242
  33.7 8.4 %collective-permute-start = (bf16[1024,128]{1,0:T(8,128)(2,1)S(1)}, bf16[1024,128]{1,0:T(8,128)(2,1)S(1)}, u32[]{:S(2)}, u32[]{:S(2)}) collective-permute-start(bf16[1024,128]{1,0:T(8,128)(2,1)S(1)} %get-tuple-element.45.kv_own), channel_id=1, source_target_pairs={{0,1},{1,0},{2,3},{3,2},{4,5},{5,4},{6,7},{7,6},{8,9},{9,8},{10,11... | collective-permute-start | bytes 786440 | tf_op jit(solution)/shard_map/ppermute | solution.py:248
  36.3 5.8 %copy-start.1 = (bf16[512,128]{1,0:T(8,128)(2,1)S(1)}, bf16[512,128]{1,0:T(8,128)(2,1)}, u32[]{:S(2)}) copy-start(bf16[512,128]{1,0:T(8,128)(2,1)} %text_k.1) | copy-start | bytes 393220
  36.3 5.8 %copy-start.2 = (bf16[512,128]{1,0:T(8,128)(2,1)S(1)}, bf16[512,128]{1,0:T(8,128)(2,1)}, u32[]{:S(2)}) copy-start(bf16[512,128]{1,0:T(8,128)(2,1)} %text_v.1) | copy-start | bytes 393220
  36.3 7.1 %collective-permute-start.6 = (bf16[1056,128]{1,0:T(8,128)(2,1)S(1)}, bf16[1056,128]{1,0:T(8,128)(2,1)S(1)}, u32[]{:S(2)}, u32[]{:S(2)}) collective-permute-start(bf16[1056,128]{1,0:T(8,128)(2,1)S(1)} %collective-permute-done.5.refs_3_), channel_id=1, source_target_pairs={{0,14},{1,15},{2,0},{3,1},{4,2},{5,3},{6,4},{7,5},{8,6},{9,7},{10,... | collective-permute-start | bytes 811016 | tf_op jit(solution)/shard_map/ppermute | solution.py:242
  42.0 8.4 %collective-permute-start.3 = (bf16[1056,128]{1,0:T(8,128)(2,1)S(1)}, bf16[1056,128]{1,0:T(8,128)(2,1)S(1)}, u32[]{:S(2)}, u32[]{:S(2)}) collective-permute-start(bf16[1056,128]{1,0:T(8,128)(2,1)S(1)} %collective-permute-done.2.refs_3_), channel_id=1, source_target_pairs={{0,2},{1,3},{2,4},{3,5},{4,6},{5,7},{6,8},{7,9},{8,10},{9,11},{10,... | collective-permute-start | bytes 811016 | tf_op jit(solution)/shard_map/ppermute | solution.py:242
  43.3 12.7 %collective-permute-start.7 = (bf16[1056,128]{1,0:T(8,128)(2,1)S(1)}, bf16[1056,128]{1,0:T(8,128)(2,1)S(1)}, u32[]{:S(2)}, u32[]{:S(2)}) collective-permute-start(bf16[1056,128]{1,0:T(8,128)(2,1)S(1)} %collective-permute-done.6.refs_3_), channel_id=1, source_target_pairs={{0,14},{1,15},{2,0},{3,1},{4,2},{5,3},{6,4},{7,5},{8,6},{9,7},{10,... | collective-permute-start | bytes 811016 | tf_op jit(solution)/shard_map/ppermute | solution.py:242
  50.4 10.3 %collective-permute-start.4 = (bf16[1056,128]{1,0:T(8,128)(2,1)S(1)}, bf16[1056,128]{1,0:T(8,128)(2,1)S(1)}, u32[]{:S(2)}, u32[]{:S(2)}) collective-permute-start(bf16[1056,128]{1,0:T(8,128)(2,1)S(1)} %collective-permute-done.3.refs_3_), channel_id=1, source_target_pairs={{0,2},{1,3},{2,4},{3,5},{4,6},{5,7},{6,8},{7,9},{8,10},{9,11},{10,... | collective-permute-start | bytes 811016 | tf_op jit(solution)/shard_map/ppermute | solution.py:242
  57.8 9.4 %collective-permute-start.9 = (bf16[1088,128]{1,0:T(8,128)(2,1)S(1)}, bf16[1088,128]{1,0:T(8,128)(2,1)S(1)}, u32[]{:S(2)}, u32[]{:S(2)}) collective-permute-start(bf16[1088,128]{1,0:T(8,128)(2,1)S(1)} %get-tuple-element.72), channel_id=1, source_target_pairs={{0,2},{1,3},{2,4},{3,5},{4,6},{5,7},{6,8},{7,9},{8,10},{9,11},{10,... | collective-permute-start | bytes 835592 | tf_op jit(solution)/shard_map/ppermute | solution.py:242
  57.9 10.7 %collective-permute-start.10 = (bf16[1088,128]{1,0:T(8,128)(2,1)S(1)}, bf16[1088,128]{1,0:T(8,128)(2,1)S(1)}, u32[]{:S(2)}, u32[]{:S(2)}) collective-permute-start(bf16[1088,128]{1,0:T(8,128)(2,1)S(1)} %get-tuple-element.73), channel_id=1, source_target_pairs={{0,14},{1,15},{2,0},{3,1},{4,2},{5,3},{6,4},{7,5},{8,6},{9,7},{10,... | collective-permute-start | bytes 835592 | tf_op jit(solution)/shard_map/ppermute | solution.py:242
  62.4 7.5 %collective-permute-start.11 = (bf16[544,128]{1,0:T(8,128)(2,1)S(1)}, bf16[544,128]{1,0:T(8,128)(2,1)S(1)}, u32[]{:S(2)}, u32[]{:S(2)}) collective-permute-start(bf16[544,128]{1,0:T(8,128)(2,1)S(1)} %get-tuple-element.75), channel_id=1, source_target_pairs={{0,12},{1,13},{2,14},{3,15},{4,0},{5,1},{6,2},{7,3},{8,4},{9,5},{1... | collective-permute-start | bytes 417800 | tf_op jit(solution)/shard_map/ppermute | solution.py:242
  65.6 12.6 %collective-permute-start.8 = (bf16[544,256]{1,0:T(8,128)(2,1)S(1)}, bf16[544,256]{1,0:T(8,128)(2,1)S(1)}, u32[]{:S(2)}, u32[]{:S(2)}) collective-permute-start(bf16[544,256]{1,0:T(8,128)(2,1)S(1)} %get-tuple-element.71), channel_id=1, source_target_pairs={{0,1},{1,0},{2,3},{3,2},{4,5},{5,4},{6,7},{7,6},{8,9},{9,8},{10,11... | collective-permute-start | bytes 835592 | tf_op jit(solution)/shard_map/ppermute | solution.py:248
  67.3 7.5 %collective-permute-start.13 = (bf16[544,128]{1,0:T(8,128)(2,1)S(1)}, bf16[544,128]{1,0:T(8,128)(2,1)S(1)}, u32[]{:S(2)}, u32[]{:S(2)}) collective-permute-start(bf16[544,128]{1,0:T(8,128)(2,1)S(1)} %shard_map.175), channel_id=1, source_target_pairs={{0,4},{1,5},{2,6},{3,7},{4,8},{5,9},{6,10},{7,11},{8,12},{9,13},{1... | collective-permute-start | bytes 417800 | tf_op jit(solution)/shard_map/ppermute | solution.py:242
  70.0 8.2 %collective-permute-start.12 = (bf16[544,128]{1,0:T(8,128)(2,1)S(1)}, bf16[544,128]{1,0:T(8,128)(2,1)S(1)}, u32[]{:S(2)}, u32[]{:S(2)}) collective-permute-start(bf16[544,128]{1,0:T(8,128)(2,1)S(1)} %shard_map.174), channel_id=1, source_target_pairs={{0,12},{1,13},{2,14},{3,15},{4,0},{5,1},{6,2},{7,3},{8,4},{9,5},{1... | collective-permute-start | bytes 417800 | tf_op jit(solution)/shard_map/ppermute | solution.py:242

commit v2 on v1

--- a/solution.py
+++ b/solution.py
@@ -50,10 +50,12 @@
     return inner // 2, lax.rem(inner, 2)
 
 
-def pack_body(q_in, k_in, v_in, o_in, g_in, logs, out, rows, q, k, v, o, g, sems):
+def pack_body(q_in, k_in, v_in, o_in, g_in, logs_in, out, rows, q, k, v, o, g, logs, sems):
     copies = [
         pltpu.make_async_copy(source, target, sems.at[n])
-        for n, (source, target) in enumerate(((g_in, g), (o_in, o), (q_in, q), (k_in, k), (v_in, v)))
+        for n, (source, target) in enumerate(
+            ((g_in, g), (o_in, o), (logs_in, logs), (q_in, q), (k_in, k), (v_in, v))
+        )
     ]
     for copy in copies:
         copy.start()
@@ -95,14 +97,16 @@
         qg[2 * NEAR + 8 * a : 2 * NEAR + 8 * a + 8, :] = total.astype(BF16)
 
 
-def one_block(q, g, logs, deltas, keys, values, dk, dv):
+def one_block(q, g, logs, deltas, keys, values, dk_in, dv_in, dk, dv):
     total = None
     for base, size in ((0, NEAR), (NEAR, 2 * OWN - NEAR)):
         k, v = keys[base : base + size, :], values[base : base + size, :]
         weights = jnp.exp2(nt(k, q) * (SCALE * LOG2E) - logs)
         mixed = (weights * (nt(v, g) - deltas)).astype(BF16)
-        dv[base : base + size, :] += nn(weights.astype(BF16), g)
-        dk[base : base + size, :] += nn(mixed, q)
+        rows = slice(base, base + size)
+        value_part, key_part = nn(weights.astype(BF16), g), nn(mixed, q)
+        dv[rows, :] = value_part if dv_in is None else dv_in[rows, :] + value_part
+        dk[rows, :] = key_part if dk_in is None else dk_in[rows, :] + key_part
         part = tn(mixed, k)
         total = part if total is None else total + part
     return total * SCALE
@@ -127,22 +131,18 @@
         target[0:NEAR, :] = kv_own[start : start + NEAR, :]
         target[NEAR : 2 * NEAR, :] = kv_other[start : start + NEAR, :]
         target[2 * NEAR : 2 * OWN, :] = text[pl.ds(pl.multiple_of(z * 64, 64), 2 * TOK), :]
-    dk[...] = jnp.zeros_like(dk)
-    dv[...] = jnp.zeros_like(dv)
     for n in range(RING):
         rows = pl.ds(pl.multiple_of(n * 64 + side * TOK, TOK), TOK)
         tq[n * TOK : (n + 1) * TOK, :] = text_q[rows, :]
         tg[n * TOK : (n + 1) * TOK, :] = text_g[rows, :]
     logs, deltas = text_ld[pl.ds(side, 1), :], text_ld[pl.ds(2 + side, 1), :]
-    dq_text[...] = one_block(tq[...], tg[...], logs, deltas, keys, values, dk, dv).astype(BF16)
+    dq_text[...] = one_block(tq[...], tg[...], logs, deltas, keys, values, None, None, dk, dv).astype(BF16)
 
 
 def own_body(keys, values, qg, dk_in, dv_in, dq, dk, dv, send):
     _, side = place()
-    dk[...] = dk_in[...]
-    dv[...] = dv_in[...]
     q, g, logs, deltas = block_operands(qg)
-    dq[...] = one_block(q, g, logs, deltas, keys, values, dk, dv)
+    dq[...] = one_block(q, g, logs, deltas, keys, values, dk_in, dv_in, dk, dv)
     text = pl.ds(pl.multiple_of(2 * NEAR + (1 - side) * TOK, TOK), TOK)
     for source, lanes, factor in ((dk, slice(0, 128), SCALE), (dv, slice(128, 256), 1.0)):
         send[0:NEAR, lanes] = (source[NEAR : 2 * NEAR, :] * factor).astype(BF16)
@@ -154,10 +154,8 @@
     first, refs = (refs[6], refs[7:]) if step == 3 else (None, refs[6:])
     dq, dk, dv = refs[:3]
     z, _ = place()
-    dk[...] = dk_in[...]
-    dv[...] = dv_in[...]
     q, g, logs, deltas = block_operands(qg)
-    dq[0:NEAR, :] = one_block(q, g, logs, deltas, keys, values, dk, dv).astype(dq.dtype)
+    dq[0:NEAR, :] = one_block(q, g, logs, deltas, keys, values, dk_in, dv_in, dk, dv).astype(dq.dtype)
     owner = lax.rem(z + offset, RING)
     text = dq_text[pl.ds(pl.multiple_of(owner * TOK, TOK), TOK), :]
     dq[NEAR:OWN, :] = text.astype(dq.dtype)
@@ -250,10 +248,10 @@
     packed = kernel(
         pack_body,
         sds((HEADS, CHUNK, 128)),
-        [HB] * 5 + [VM],
+        [HB] * 6,
         scratch=[pltpu.VMEM((HEADS, 8, 128), F32)]
         + [pltpu.VMEM((TOK, HEADS * 128), BF16)] * 5
-        + [pltpu.SemaphoreType.DMA((5,))],
+        + [pltpu.VMEM((HEADS, TOK), F32), pltpu.SemaphoreType.DMA((6,))],
         limit=WHOLE_VMEM,
     )(query_image, key_image, value_image, attended_image, upstream_image, logsum_image.T)
     got = exchanged(packed)

time: 96.2 us -> 95.4 us (level)
  no operation moved by 1% of the time
where the time goes in v2:
time: 95.4 us; the launch traced here: 95.2 us
  blocking collectives  34.7 us (36%)
  starting transfers between devices  23.6 us (25%)
  Pallas kernels  19.1 us (20%)
  waiting for transfers between devices  16.5 us (17%)
    all_to_all x2, blocking collectives, exchanged(): return lax.all_to_all(x, 'outer', split_axis=0, concat_axis=0, tiled=True)  34.7 us
    ppermute x12, starting transfers between devices, along_ring(): return lax.ppermute(x, 'inner', pairs)  19.6 us
    ppermute x12, waiting for transfers between devices, along_ring(): return lax.ppermute(x, 'inner', pairs)  16.5 us
    pallas_call x7, Pallas kernels, shards(): kernel(functools.partial(far_body, step, step if n else RING - step), [pa...  12.5 us
    ppermute x2, starting transfers between devices, across(): return lax.ppermute(x, 'inner', [(n, n ^ 1) for n in range(2 * RING)])  4.06 us
    pallas_call x1, Pallas kernels, shards(): kernel(pack_body, sds((HEADS, CHUNK, 128)), [HB] * 6, scratch=[pltpu.VMEM...  2.28 us
  transfers between devices with their start and end apart: 14, of which 6 were waited for; matrix products, arithmetic and copies ran while one was open for 0% of the time, Pallas kernels for 16%

profile of v2, /device:TPU:1, one launch (start us, length us, event | category | flops | bytes accessed | tf_op | source)
XLA Modules:
  0.0 95.2 jit_solution(17375181626984490691)
XLA Ops:
  0.6 2.3 %shard_map.163 = bf16[16,136,128]{2,1,0:T(8,128)(2,1)} custom-call(bf16[32,2048]{1,0:T(8,128)(2,1)} %q_in.1, bf16[32,2048]{1,0:T(8,128)(2,1)} %k_in.1, bf16[32,2048]{1,0:T(8,128)(2,1)} %v_in.1, bf16[32,2048]{1,0:T(8,128)(2,1)} %o_in.1, bf16[32,2048]{1,0:T(8,128)(2,1)} %g_in.1, f32[16,32]{1,0:T(8,128)} %bitcast.5), custom_call_target="tpu_custom_call" | custom-call | bytes 1048576 | tf_op jit(solution)/shard_map/pallas_call | solution.py:248
  2.9 17.9 %all_to_all.10.got = bf16[16,136,128]{2,1,0:T(8,128)(2,1)S(1)} all-to-all(bf16[16,136,128]{2,1,0:T(8,128)(2,1)} %shard_map.163), channel_id=1, replica_groups=mesh['outer'=16,'inner'=16] {'outer'}, dimensions={0} | all-to-all | bytes 1114112 | tf_op jit(solution)/shard_map/all_to_all | solution.py:243
  20.9 0.0 copy-start.5
  20.9 1.7 %collective-permute-start.1 = (bf16[1056,128]{1,0:T(8,128)(2,1)S(1)}, bf16[1056,128]{1,0:T(8,128)(2,1)S(1)}, u32[]{:S(2)}, u32[]{:S(2)}) collective-permute-start(bf16[1056,128]{1,0:T(8,128)(2,1)S(1)} %get-tuple-element.48.qg), channel_id=1, source_target_pairs={{0,2},{1,3},{2,4},{3,5},{4,6},{5,7},{6,8},{7,9},{8,10},{9,11},{10,... | collective-permute-start | bytes 811016 | tf_op jit(solution)/shard_map/ppermute | solution.py:240
  22.6 4.0 %collective-permute-start.5 = (bf16[1056,128]{1,0:T(8,128)(2,1)S(1)}, bf16[1056,128]{1,0:T(8,128)(2,1)S(1)}, u32[]{:S(2)}, u32[]{:S(2)}) collective-permute-start(bf16[1056,128]{1,0:T(8,128)(2,1)S(1)} %get-tuple-element.48.qg), channel_id=1, source_target_pairs={{0,14},{1,15},{2,0},{3,1},{4,2},{5,3},{6,4},{7,5},{8,6},{9,7},{10,... | collective-permute-start | bytes 811016 | tf_op jit(solution)/shard_map/ppermute | solution.py:240
  26.7 6.4 %collective-permute-done.1.refs_3_ = bf16[1056,128]{1,0:T(8,128)(2,1)S(1)} collective-permute-done((bf16[1056,128]{1,0:T(8,128)(2,1)S(1)}, bf16[1056,128]{1,0:T(8,128)(2,1)S(1)}, u32[]{:S(2)}, u32[]{:S(2)}) %collective-permute-start.1) | collective-permute-done | bytes 270368 | tf_op jit(solution)/shard_map/ppermute | solution.py:240
  33.0 0.0 collective-permute-start.2
  33.0 2.5 %collective-permute-start = (bf16[1024,128]{1,0:T(8,128)(2,1)S(1)}, bf16[1024,128]{1,0:T(8,128)(2,1)S(1)}, u32[]{:S(2)}, u32[]{:S(2)}) collective-permute-start(bf16[1024,128]{1,0:T(8,128)(2,1)S(1)} %get-tuple-element.45.kv_own), channel_id=1, source_target_pairs={{0,1},{1,0},{2,3},{3,2},{4,5},{5,4},{6,7},{7,6},{8,9},{9,8},{10,11... | collective-permute-start | bytes 786440 | tf_op jit(solution)/shard_map/ppermute | solution.py:246
  35.5 0.1 mul.22
  35.6 0.0 collective-permute-done.5.refs_3_
  35.6 2.7 %collective-permute-start.6 = (bf16[1056,128]{1,0:T(8,128)(2,1)S(1)}, bf16[1056,128]{1,0:T(8,128)(2,1)S(1)}, u32[]{:S(2)}, u32[]{:S(2)}) collective-permute-start(bf16[1056,128]{1,0:T(8,128)(2,1)S(1)} %collective-permute-done.5.refs_3_), channel_id=1, source_target_pairs={{0,14},{1,15},{2,0},{3,1},{4,2},{5,3},{6,4},{7,5},{8,6},{9,7},{10,... | collective-permute-start | bytes 811016 | tf_op jit(solution)/shard_map/ppermute | solution.py:240
  38.4 0.1 multiply_reduce_fusion
  38.5 0.1 stack.7
  38.6 2.7 %collective-permute-done.2.refs_3_ = bf16[1056,128]{1,0:T(8,128)(2,1)S(1)} collective-permute-done((bf16[1056,128]{1,0:T(8,128)(2,1)S(1)}, bf16[1056,128]{1,0:T(8,128)(2,1)S(1)}, u32[]{:S(2)}, u32[]{:S(2)}) %collective-permute-start.2) | collective-permute-done | bytes 270368 | tf_op jit(solution)/shard_map/ppermute | solution.py:240
  41.3 0.0 collective-permute-start.3
  41.3 0.1 reshape.32.text_ld
  41.4 0.0 collective-permute-done.kv_other
  41.4 0.9 shard_map.165
  42.4 0.3 collective-permute-done.6.refs_3_
  42.7 3.4 %collective-permute-start.7 = (bf16[1056,128]{1,0:T(8,128)(2,1)S(1)}, bf16[1056,128]{1,0:T(8,128)(2,1)S(1)}, u32[]{:S(2)}, u32[]{:S(2)}) collective-permute-start(bf16[1056,128]{1,0:T(8,128)(2,1)S(1)} %collective-permute-done.6.refs_3_), channel_id=1, source_target_pairs={{0,14},{1,15},{2,0},{3,1},{4,2},{5,3},{6,4},{7,5},{8,6},{9,7},{10,... | collective-permute-start | bytes 811016 | tf_op jit(solution)/shard_map/ppermute | solution.py:240
  46.1 1.8 %shard_map.166 = (bf16[544,128]{1,0:T(8,128)(2,1)S(1)}, f32[1088,128]{1,0:T(8,128)S(1)}, f32[1088,128]{1,0:T(8,128)S(1)}) custom-call(bf16[1088,128]{1,0:T(8,128)(2,1)S(1)} %get-tuple-element.46.refs_0_.keys, bf16[1088,128]{1,0:T(8,128)(2,1)S(1)} %get-tuple-element.47.refs_1_.values, ...), custom_call_target="tpu_custom_call", output_to_operand_aliasing={{1}: (4, {}), {2}: (5, {})} | custom-call | flops 713031680 | bytes 1048576 | tf_op jit(solution)/shard_map/pallas_call | solution.py:283
  47.9 1.8 %shard_map.167 = (bf16[544,128]{1,0:T(8,128)(2,1)S(1)}, f32[1088,128]{1,0:T(8,128)S(1)}, f32[1088,128]{1,0:T(8,128)S(1)}) custom-call(bf16[1088,128]{1,0:T(8,128)(2,1)S(1)} %get-tuple-element.46.refs_0_.keys, bf16[1088,128]{1,0:T(8,128)(2,1)S(1)} %get-tuple-element.47.refs_1_.values, ...), custom_call_target="tpu_custom_call", output_to_operand_aliasing={{1}: (4, {}), {2}: (5, {})} | custom-call | flops 713031680 | bytes 1048576 | tf_op jit(solution)/shard_map/pallas_call | solution.py:283
  49.7 0.0 collective-permute-done.3.refs_3_
  49.7 0.3 collective-permute-start.4
  50.0 1.8 %shard_map.168 = (f32[544,128]{1,0:T(8,128)S(1)}, f32[1088,128]{1,0:T(8,128)S(1)}, f32[1088,128]{1,0:T(8,128)S(1)}) custom-call(bf16[1088,128]{1,0:T(8,128)(2,1)S(1)} %get-tuple-element.46.refs_0_.keys, bf16[1088,128]{1,0:T(8,128)(2,1)S(1)} %get-tuple-element.47.refs_1_.values, ...), custom_call_target="tpu_custom_call", output_to_operand_aliasing={{1}: (4, {}), {2}: (5, {})} | custom-call | flops 713031680 | bytes 1048576 | tf_op jit(solution)/shard_map/pallas_call | solution.py:283
  51.8 1.8 %shard_map.169 = (f32[544,128]{1,0:T(8,128)S(1)}, f32[1088,128]{1,0:T(8,128)S(1)}, f32[1088,128]{1,0:T(8,128)S(1)}) custom-call(bf16[1088,128]{1,0:T(8,128)(2,1)S(1)} %get-tuple-element.46.refs_0_.keys, bf16[1088,128]{1,0:T(8,128)(2,1)S(1)} %get-tuple-element.47.refs_1_.values, ...), custom_call_target="tpu_custom_call", output_to_operand_aliasing={{1}: (4, {}), {2}: (5, {})} | custom-call | flops 713031680 | bytes 1048576 | tf_op jit(solution)/shard_map/pallas_call | solution.py:283
  53.5 1.8 %shard_map.170 = (bf16[1088,128]{1,0:T(8,128)(2,1)S(1)}, f32[1088,128]{1,0:T(8,128)S(1)}, f32[1088,128]{1,0:T(8,128)S(1)}) custom-call(bf16[1088,128]{1,0:T(8,128)(2,1)S(1)} %get-tuple-element.46.refs_0_.keys, bf16[1088,128]{1,0:T(8,128)(2,1)S(1)} %get-tuple-element.47.refs_1_.values, ...), custom_call_target="tpu_custom_call", output_to_operand_aliasing={{1}: (4, {}), {2}: (5, {})} | custom-call | flops 713031680 | bytes 1048576 | tf_op jit(solution)/shard_map/pallas_call | solution.py:283
  55.3 0.0 collective-permute-done.7.refs_3_
  55.4 1.8 %shard_map.171 = (bf16[1088,128]{1,0:T(8,128)(2,1)S(1)}, f32[1088,128]{1,0:T(8,128)S(1)}, f32[1088,128]{1,0:T(8,128)S(1)}) custom-call(bf16[1088,128]{1,0:T(8,128)(2,1)S(1)} %get-tuple-element.46.refs_0_.keys, bf16[1088,128]{1,0:T(8,128)(2,1)S(1)} %get-tuple-element.47.refs_1_.values, ...), custom_call_target="tpu_custom_call", output_to_operand_aliasing={{1}: (4, {}), {2}: (5, {})} | custom-call | flops 713031680 | bytes 1048576 | tf_op jit(solution)/shard_map/pallas_call | solution.py:283
  57.1 0.1 collective-permute-start.9
  57.2 2.7 %collective-permute-start.10 = (bf16[1088,128]{1,0:T(8,128)(2,1)S(1)}, bf16[1088,128]{1,0:T(8,128)(2,1)S(1)}, u32[]{:S(2)}, u32[]{:S(2)}) collective-permute-start(bf16[1088,128]{1,0:T(8,128)(2,1)S(1)} %get-tuple-element.73), channel_id=1, source_target_pairs={{0,14},{1,15},{2,0},{3,1},{4,2},{5,3},{6,4},{7,5},{8,6},{9,7},{10,... | collective-permute-start | bytes 835592 | tf_op jit(solution)/shard_map/ppermute | solution.py:240
  60.0 0.0 collective-permute-done.4.refs_3_
  60.0 1.8 %shard_map.172 = (bf16[544,128]{1,0:T(8,128)(2,1)S(1)}, f32[1088,128]{1,0:T(8,128)S(1)}, f32[1088,128]{1,0:T(8,128)S(1)}) custom-call(bf16[1088,128]{1,0:T(8,128)(2,1)S(1)} %get-tuple-element.46.refs_0_.keys, bf16[1088,128]{1,0:T(8,128)(2,1)S(1)} %get-tuple-element.47.refs_1_.values, ...), custom_call_target="tpu_custom_call", output_to_operand_aliasing={{1}: (4, {}), {2}: (5, {})} | custom-call | flops 713031680 | bytes 1048576 | tf_op jit(solution)/shard_map/pallas_call | solution.py:283
  61.8 1.2 %collective-permute-start.11 = (bf16[544,128]{1,0:T(8,128)(2,1)S(1)}, bf16[544,128]{1,0:T(8,128)(2,1)S(1)}, u32[]{:S(2)}, u32[]{:S(2)}) collective-permute-start(bf16[544,128]{1,0:T(8,128)(2,1)S(1)} %get-tuple-element.75), channel_id=1, source_target_pairs={{0,12},{1,13},{2,14},{3,15},{4,0},{5,1},{6,2},{7,3},{8,4},{9,5},{1... | collective-permute-start | bytes 417800 | tf_op jit(solution)/shard_map/ppermute | solution.py:240
  62.9 1.8 %shard_map.173 = (f32[512,128]{1,0:T(8,128)S(1)}, f32[1088,128]{1,0:T(8,128)S(1)}, f32[1088,128]{1,0:T(8,128)S(1)}, bf16[544,256]{1,0:T(8,128)(2,1)S(1)}) custom-call(bf16[1088,128]{1,0:T(8,128)(2,1)S(1)} %get-tuple-element.46.refs_0_.keys, bf16[1088,128]{1,0:T(8,128)(2,1)S(1)} %get-tuple-element.47.refs_1_.values, ...), custom_call_target="tpu_custom_call", output_to_operand_aliasing={{1}: (3, {}), {2}: (4, {})} | custom-call | flops 713031680 | bytes 1048576 | tf_op jit(solution)/shard_map/pallas_call | solution.py:292
  64.7 1.6 %collective-permute-start.8 = (bf16[544,256]{1,0:T(8,128)(2,1)S(1)}, bf16[544,256]{1,0:T(8,128)(2,1)S(1)}, u32[]{:S(2)}, u32[]{:S(2)}) collective-permute-start(bf16[544,256]{1,0:T(8,128)(2,1)S(1)} %get-tuple-element.71), channel_id=1, source_target_pairs={{0,1},{1,0},{2,3},{3,2},{4,5},{5,4},{6,7},{7,6},{8,9},{9,8},{10,11... | collective-permute-start | bytes 835592 | tf_op jit(solution)/shard_map/ppermute | solution.py:246
  66.3 0.0 collective-permute-done.9.refs_0_.from_low
  66.4 1.3 %collective-permute-start.13 = (bf16[544,128]{1,0:T(8,128)(2,1)S(1)}, bf16[544,128]{1,0:T(8,128)(2,1)S(1)}, u32[]{:S(2)}, u32[]{:S(2)}) collective-permute-start(bf16[544,128]{1,0:T(8,128)(2,1)S(1)} %shard_map.175), channel_id=1, source_target_pairs={{0,4},{1,5},{2,6},{3,7},{4,8},{5,9},{6,10},{7,11},{8,12},{9,13},{1... | collective-permute-start | bytes 417800 | tf_op jit(solution)/shard_map/ppermute | solution.py:240
  67.7 0.0 collective-permute-done.10.refs_0_.from_high
  67.7 0.8 collective-permute-done.11.refs_1_
  68.5 0.1 shard_map.174
  68.6 2.1 %collective-permute-start.12 = (bf16[544,128]{1,0:T(8,128)(2,1)S(1)}, bf16[544,128]{1,0:T(8,128)(2,1)S(1)}, u32[]{:S(2)}, u32[]{:S(2)}) collective-permute-start(bf16[544,128]{1,0:T(8,128)(2,1)S(1)} %shard_map.174), channel_id=1, source_target_pairs={{0,12},{1,13},{2,14},{3,15},{4,0},{5,1},{6,2},{7,3},{8,4},{9,5},{1... | collective-permute-start | bytes 417800 | tf_op jit(solution)/shard_map/ppermute | solution.py:240
  70.7 3.2 %collective-permute-done.13.refs_1_ = bf16[544,128]{1,0:T(8,128)(2,1)S(1)} collective-permute-done((bf16[544,128]{1,0:T(8,128)(2,1)S(1)}, bf16[544,128]{1,0:T(8,128)(2,1)S(1)}, u32[]{:S(2)}, u32[]{:S(2)}) %collective-permute-start.13) | collective-permute-done | bytes 139296 | tf_op jit(solution)/shard_map/ppermute | solution.py:240
  73.9 3.1 %collective-permute-done.12.refs_0_ = bf16[544,128]{1,0:T(8,128)(2,1)S(1)} collective-permute-done((bf16[544,128]{1,0:T(8,128)(2,1)S(1)}, bf16[544,128]{1,0:T(8,128)(2,1)S(1)}, u32[]{:S(2)}, u32[]{:S(2)}) %collective-permute-start.12) | collective-permute-done | bytes 139296 | tf_op jit(solution)/shard_map/ppermute | solution.py:240
  76.9 0.0 collective-permute-done.8.kv_got
  76.9 0.6 shard_map.176
  77.6 16.8 %all_to_all.11.got = bf16[16,96,128]{2,1,0:T(8,128)(2,1)S(1)} all-to-all(bf16[16,96,128]{2,1,0:T(8,128)(2,1)S(1)} %get-tuple-element.77), channel_id=1, replica_groups=mesh['outer'=16,'inner'=16] {'outer'}, dimensions={0} | all-to-all | bytes 786432 | tf_op jit(solution)/shard_map/all_to_all | solution.py:243
  94.4 0.8 shard_map.177
  (16 shorter events, 0.1 us)
Async XLA Ops:
  20.9 17.5 %copy-start = (bf16[512,128]{1,0:T(8,128)(2,1)S(1)}, bf16[512,128]{1,0:T(8,128)(2,1)}, u32[]{:S(2)}) copy-start(bf16[512,128]{1,0:T(8,128)(2,1)} %text_g.1) | copy-start | bytes 393220
  20.9 17.5 %copy-start.4 = (bf16[512,128]{1,0:T(8,128)(2,1)S(1)}, bf16[512,128]{1,0:T(8,128)(2,1)}, u32[]{:S(2)}) copy-start(bf16[512,128]{1,0:T(8,128)(2,1)} %param.21) | copy-start | bytes 393220
  20.9 20.6 %copy-start.3 = (bf16[512,128]{1,0:T(8,128)(2,1)S(1)}, bf16[512,128]{1,0:T(8,128)(2,1)}, u32[]{:S(2)}) copy-start(bf16[512,128]{1,0:T(8,128)(2,1)} %text_q.1) | copy-start | bytes 393220
  20.9 14.6 %copy-start.5 = (f32[512,1]{0,1:T(1,128)S(1)}, f32[512,1]{0,1:T(1,128)}, u32[]{:S(2)}) copy-start(f32[512,1]{0,1:T(1,128)} %param.23) | copy-start | bytes 6148
  20.9 12.1 %collective-permute-start.1 = (bf16[1056,128]{1,0:T(8,128)(2,1)S(1)}, bf16[1056,128]{1,0:T(8,128)(2,1)S(1)}, u32[]{:S(2)}, u32[]{:S(2)}) collective-permute-start(bf16[1056,128]{1,0:T(8,128)(2,1)S(1)} %get-tuple-element.48.qg), channel_id=1, source_target_pairs={{0,2},{1,3},{2,4},{3,5},{4,6},{5,7},{6,8},{7,9},{8,10},{9,11},{10,... | collective-permute-start | bytes 811016 | tf_op jit(solution)/shard_map/ppermute | solution.py:240
  22.6 13.0 %collective-permute-start.5 = (bf16[1056,128]{1,0:T(8,128)(2,1)S(1)}, bf16[1056,128]{1,0:T(8,128)(2,1)S(1)}, u32[]{:S(2)}, u32[]{:S(2)}) collective-permute-start(bf16[1056,128]{1,0:T(8,128)(2,1)S(1)} %get-tuple-element.48.qg), channel_id=1, source_target_pairs={{0,14},{1,15},{2,0},{3,1},{4,2},{5,3},{6,4},{7,5},{8,6},{9,7},{10,... | collective-permute-start | bytes 811016 | tf_op jit(solution)/shard_map/ppermute | solution.py:240
  33.0 8.3 %collective-permute-start.2 = (bf16[1056,128]{1,0:T(8,128)(2,1)S(1)}, bf16[1056,128]{1,0:T(8,128)(2,1)S(1)}, u32[]{:S(2)}, u32[]{:S(2)}) collective-permute-start(bf16[1056,128]{1,0:T(8,128)(2,1)S(1)} %collective-permute-done.1.refs_3_), channel_id=1, source_target_pairs={{0,2},{1,3},{2,4},{3,5},{4,6},{5,7},{6,8},{7,9},{8,10},{9,11},{10,... | collective-permute-start | bytes 811016 | tf_op jit(solution)/shard_map/ppermute | solution.py:240
  33.0 8.4 %collective-permute-start = (bf16[1024,128]{1,0:T(8,128)(2,1)S(1)}, bf16[1024,128]{1,0:T(8,128)(2,1)S(1)}, u32[]{:S(2)}, u32[]{:S(2)}) collective-permute-start(bf16[1024,128]{1,0:T(8,128)(2,1)S(1)} %get-tuple-element.45.kv_own), channel_id=1, source_target_pairs={{0,1},{1,0},{2,3},{3,2},{4,5},{5,4},{6,7},{7,6},{8,9},{9,8},{10,11... | collective-permute-start | bytes 786440 | tf_op jit(solution)/shard_map/ppermute | solution.py:246
  35.6 5.8 %copy-start.1 = (bf16[512,128]{1,0:T(8,128)(2,1)S(1)}, bf16[512,128]{1,0:T(8,128)(2,1)}, u32[]{:S(2)}) copy-start(bf16[512,128]{1,0:T(8,128)(2,1)} %text_k.1) | copy-start | bytes 393220
  35.6 5.8 %copy-start.2 = (bf16[512,128]{1,0:T(8,128)(2,1)S(1)}, bf16[512,128]{1,0:T(8,128)(2,1)}, u32[]{:S(2)}) copy-start(bf16[512,128]{1,0:T(8,128)(2,1)} %text_v.1) | copy-start | bytes 393220
  35.6 7.1 %collective-permute-start.6 = (bf16[1056,128]{1,0:T(8,128)(2,1)S(1)}, bf16[1056,128]{1,0:T(8,128)(2,1)S(1)}, u32[]{:S(2)}, u32[]{:S(2)}) collective-permute-start(bf16[1056,128]{1,0:T(8,128)(2,1)S(1)} %collective-permute-done.5.refs_3_), channel_id=1, source_target_pairs={{0,14},{1,15},{2,0},{3,1},{4,2},{5,3},{6,4},{7,5},{8,6},{9,7},{10,... | collective-permute-start | bytes 811016 | tf_op jit(solution)/shard_map/ppermute | solution.py:240
  41.3 8.4 %collective-permute-start.3 = (bf16[1056,128]{1,0:T(8,128)(2,1)S(1)}, bf16[1056,128]{1,0:T(8,128)(2,1)S(1)}, u32[]{:S(2)}, u32[]{:S(2)}) collective-permute-start(bf16[1056,128]{1,0:T(8,128)(2,1)S(1)} %collective-permute-done.2.refs_3_), channel_id=1, source_target_pairs={{0,2},{1,3},{2,4},{3,5},{4,6},{5,7},{6,8},{7,9},{8,10},{9,11},{10,... | collective-permute-start | bytes 811016 | tf_op jit(solution)/shard_map/ppermute | solution.py:240
  42.7 12.7 %collective-permute-start.7 = (bf16[1056,128]{1,0:T(8,128)(2,1)S(1)}, bf16[1056,128]{1,0:T(8,128)(2,1)S(1)}, u32[]{:S(2)}, u32[]{:S(2)}) collective-permute-start(bf16[1056,128]{1,0:T(8,128)(2,1)S(1)} %collective-permute-done.6.refs_3_), channel_id=1, source_target_pairs={{0,14},{1,15},{2,0},{3,1},{4,2},{5,3},{6,4},{7,5},{8,6},{9,7},{10,... | collective-permute-start | bytes 811016 | tf_op jit(solution)/shard_map/ppermute | solution.py:240
  49.7 10.3 %collective-permute-start.4 = (bf16[1056,128]{1,0:T(8,128)(2,1)S(1)}, bf16[1056,128]{1,0:T(8,128)(2,1)S(1)}, u32[]{:S(2)}, u32[]{:S(2)}) collective-permute-start(bf16[1056,128]{1,0:T(8,128)(2,1)S(1)} %collective-permute-done.3.refs_3_), channel_id=1, source_target_pairs={{0,2},{1,3},{2,4},{3,5},{4,6},{5,7},{6,8},{7,9},{8,10},{9,11},{10,... | collective-permute-start | bytes 811016 | tf_op jit(solution)/shard_map/ppermute | solution.py:240
  57.1 9.2 %collective-permute-start.9 = (bf16[1088,128]{1,0:T(8,128)(2,1)S(1)}, bf16[1088,128]{1,0:T(8,128)(2,1)S(1)}, u32[]{:S(2)}, u32[]{:S(2)}) collective-permute-start(bf16[1088,128]{1,0:T(8,128)(2,1)S(1)} %get-tuple-element.72), channel_id=1, source_target_pairs={{0,2},{1,3},{2,4},{3,5},{4,6},{5,7},{6,8},{7,9},{8,10},{9,11},{10,... | collective-permute-start | bytes 835592 | tf_op jit(solution)/shard_map/ppermute | solution.py:240
  57.2 10.5 %collective-permute-start.10 = (bf16[1088,128]{1,0:T(8,128)(2,1)S(1)}, bf16[1088,128]{1,0:T(8,128)(2,1)S(1)}, u32[]{:S(2)}, u32[]{:S(2)}) collective-permute-start(bf16[1088,128]{1,0:T(8,128)(2,1)S(1)} %get-tuple-element.73), channel_id=1, source_target_pairs={{0,14},{1,15},{2,0},{3,1},{4,2},{5,3},{6,4},{7,5},{8,6},{9,7},{10,... | collective-permute-start | bytes 835592 | tf_op jit(solution)/shard_map/ppermute | solution.py:240
  61.8 6.8 %collective-permute-start.11 = (bf16[544,128]{1,0:T(8,128)(2,1)S(1)}, bf16[544,128]{1,0:T(8,128)(2,1)S(1)}, u32[]{:S(2)}, u32[]{:S(2)}) collective-permute-start(bf16[544,128]{1,0:T(8,128)(2,1)S(1)} %get-tuple-element.75), channel_id=1, source_target_pairs={{0,12},{1,13},{2,14},{3,15},{4,0},{5,1},{6,2},{7,3},{8,4},{9,5},{1... | collective-permute-start | bytes 417800 | tf_op jit(solution)/shard_map/ppermute | solution.py:240
  64.7 12.2 %collective-permute-start.8 = (bf16[544,256]{1,0:T(8,128)(2,1)S(1)}, bf16[544,256]{1,0:T(8,128)(2,1)S(1)}, u32[]{:S(2)}, u32[]{:S(2)}) collective-permute-start(bf16[544,256]{1,0:T(8,128)(2,1)S(1)} %get-tuple-element.71), channel_id=1, source_target_pairs={{0,1},{1,0},{2,3},{3,2},{4,5},{5,4},{6,7},{7,6},{8,9},{9,8},{10,11... | collective-permute-start | bytes 835592 | tf_op jit(solution)/shard_map/ppermute | solution.py:246
  66.4 7.5 %collective-permute-start.13 = (bf16[544,128]{1,0:T(8,128)(2,1)S(1)}, bf16[544,128]{1,0:T(8,128)(2,1)S(1)}, u32[]{:S(2)}, u32[]{:S(2)}) collective-permute-start(bf16[544,128]{1,0:T(8,128)(2,1)S(1)} %shard_map.175), channel_id=1, source_target_pairs={{0,4},{1,5},{2,6},{3,7},{4,8},{5,9},{6,10},{7,11},{8,12},{9,13},{1... | collective-permute-start | bytes 417800 | tf_op jit(solution)/shard_map/ppermute | solution.py:240
  68.6 8.3 %collective-permute-start.12 = (bf16[544,128]{1,0:T(8,128)(2,1)S(1)}, bf16[544,128]{1,0:T(8,128)(2,1)S(1)}, u32[]{:S(2)}, u32[]{:S(2)}) collective-permute-start(bf16[544,128]{1,0:T(8,128)(2,1)S(1)} %shard_map.174), channel_id=1, source_target_pairs={{0,12},{1,13},{2,14},{3,15},{4,0},{5,1},{6,2},{7,3},{8,4},{9,5},{1... | collective-permute-start | bytes 417800 | tf_op jit(solution)/shard_map/ppermute | solution.py:240
